TPU v7x, 32 devices: a whole 2x2x4 slice. The times are simulated.
32 devices in a mesh: gx: 4 (over y, x), gy: 4 (over z), gz: 2 (over core).
Axes of the slice: x: 2, y: 2, z: 4, core: 2. Of those that a mesh axis runs over, the one named last changes fastest.
Arguments:
- displacement: float32 [4, 4, 9216], P('gx', 'gy', 'gz'), may hold values from -0.1 to 0.1
- species: int32 [4, 4, 3072], P('gx', 'gy', 'gz'), may hold values from 0 to 1
- centres: int32 [4, 4, 32], P('gx', 'gy', 'gz'), may hold values from 0 to 1535, as said below
- neighbours: int32 [4, 4, 1024], P('gx', 'gy', 'gz'), may hold values from 0 to 5183, as said below
- neighbour_count: int32 [4, 4, 32], P('gx', 'gy', 'gz'), may hold values from 1 to 32, as said below
- live_centres: int32 [4, 4, 2], P('gx', 'gy', 'gz'), may hold values from 8 to 16, as said below
- w_two: float32 [12, 64], replicated, may hold values from -1.75 to 1.75
- w_lat: float32 [64, 64], replicated, may hold values from -0.75 to 0.75
- w_env: float32 [64, 64], replicated, may hold values from -0.75 to 0.75
- w_out: float32 [256, 64], replicated, may hold values from -0.375 to 0.375
- readout: float32 [64], replicated, may hold values from -0.75 to 0.75
Outputs:
- centre_energy: float32 [4, 4, 32], P('gx', 'gy', 'gz')
- forces: float32 [4, 4, 9216], P('gx', 'gy', 'gz')
Inputs may be any that keep to these rules, and one draw needn't show every extreme that they name: `centres`: local atom index of an owned atom; entries may repeat. `neighbours`: extended index of an atom whose cell lies within two cells of the centre's cell in each dimension, with squared cell distance at most 4; never the centre itself. `neighbour_count`: in every domain some centre has all 32 slots live. `live_centres`: some domain has all 16 centres live; the live centres are the first ones.
All inputs are finite; a program needn't handle non-finite values.
Results may differ from a plain program's by a relative error of at most 0.0003.
Values sent between devices are 32-bit elements; how exact they have to be, the bound alone decides.
A program may use at most 64 MiB of HBM per device.

v0:
```python
import math

import jax
import jax.numpy as jnp
from jax import lax
from jax.experimental import pallas as pl
from jax.experimental.pallas import tpu as pltpu
from jax.sharding import PartitionSpec as P

CELLS = 8
NBASIS = 8
CUTOFF = 6.0
SIDE = 3.1
ENV = 0.2
LANES = 128
ZROWS = CELLS * 9
KINDS = CELLS * 3
AXES = ("gx", "gy", "gz")

NN = (((1,), (0,)), ((), ()))
NT = (((1,), (1,)), ((), ()))


def halves(x):
    hi = x.astype(jnp.bfloat16)
    lo = (x - hi.astype(jnp.float32)).astype(jnp.bfloat16)
    return hi, lo


def raw(a, b, dims):
    return lax.dot_general(a, b, dims, preferred_element_type=jnp.float32)


def mm(a, b, dims=NN):
    ah, al = a if isinstance(a, tuple) else halves(a)
    bh, bl = b if isinstance(b, tuple) else halves(b)
    if dims is NT:
        m, n = ah.shape[0], bh.shape[0]
        both = raw(jnp.concatenate([ah, al], axis=0), jnp.concatenate([bh, bl], axis=0), NT)
        return both[:m, :n] + (both[:m, n:] + both[m:, :n])
    if ah.shape[1] > 2 * LANES - 1:
        return raw(ah, bh, dims) + (raw(ah, bl, dims) + raw(al, bh, dims))
    return raw(
        jnp.concatenate([ah, ah, al], axis=1), jnp.concatenate([bh, bl, bh], axis=0), NN
    )


def mm_exact_b(a, b, dims=NN):
    ah, al = halves(a)
    return raw(ah, b, dims) + raw(al, b, dims)


def mm_exact_a(a, b):
    n = b.shape[0]
    both = raw(a, jnp.concatenate(halves(b), axis=0), NT)
    return both[:, :n] + both[:, n:]


def slot_plan(depth):
    plan = []
    tile = CELLS
    for dz in [0, 1] if depth == 2 else [0, 1, -1]:
        for dx in (-1, 0, 1):
            for dy in (-1, 0, 1):
                if dx == dy == dz == 0:
                    continue
                if dx == 0 and dy == 0:
                    tiles = CELLS
                elif dz == 0 and (dx == 0 or dy == 0):
                    tiles = 2
                else:
                    tiles = 1
                plan.append((dx, dy, dz, tile, tiles))
                tile += tiles
    return plan, tile


def origin(step, tiles):
    return 0 if step >= 0 else CELLS - tiles


def wave(turns):
    f = turns - jnp.floor(turns + 0.5)
    f = jnp.where(f > 0.25, 0.5 - f, jnp.where(f < -0.25, -0.5 - f, f))
    x = f * (2.0 * math.pi)
    s = x * x
    p = -1.0 / 39916800.0
    for c in (1.0 / 362880.0, -1.0 / 5040.0, 1.0 / 120.0, -1.0 / 6.0):
        p = p * s + c
    return x + x * s * p


def divided(value, by):
    return jnp.floor((value + 0.5) * (1.0 / by))


def silu_pair(x):
    s = 1.0 / (1.0 + jnp.exp(-x))
    return x * s, s * (1.0 + x * (1.0 - s))


def kernel_body(sizes, plan, disp_hbm, spec_hbm, cen_hbm, nbr_hbm, cnt_hbm, alive_hbm, two_hbm,
                lat_hbm, env_hbm, out_hbm, readout_hbm, result,
                disp, spec, cen, nbr, cnt, alive, w_two, w_lat, w_env, w_out_t, readout,
                table, pack, part, got, send_a, recv_a, send_b, recv_b, load):
    loads = [
        pltpu.make_async_copy(src, dst, load.at[at])
        for at, (src, dst) in enumerate(
            (
                (disp_hbm, disp),
                (spec_hbm, spec),
                (cen_hbm, cen),
                (nbr_hbm, nbr),
                (cnt_hbm, cnt),
                (alive_hbm, alive),
                (two_hbm, w_two),
                (lat_hbm, w_lat),
                (env_hbm, w_env),
                (out_hbm, w_out_t),
                (readout_hbm, readout),
            )
        )
    ]
    for copy in loads:
        copy.start()
    disp, spec, cen, nbr, cnt, alive = (
        ref.at[0] for ref in (disp, spec, cen, nbr, cnt, alive)
    )
    total = result.at[pl.ds(0, CELLS * CELLS)]
    me = tuple(lax.axis_index(a) for a in AXES)

    def peer(step, sign):
        return tuple(
            lax.rem(i + (sign * d + n), n) if d else i for i, d, n in zip(me, step, sizes)
        )

    barrier = pltpu.get_barrier_semaphore()
    for slot in plan:
        pl.semaphore_signal(
            barrier, inc=1, device_id=peer(slot[:3], 1), device_id_type=pl.DeviceIdType.MESH
        )

    for copy in loads[:2]:
        copy.wait()
    dwide, swide = 16 * ZROWS, 16 * KINDS
    dline = jnp.concatenate([disp[:, dwide * q : dwide * (q + 1)] for q in range(4)], axis=0)
    sline = jnp.concatenate([spec[:, swide * q : swide * (q + 1)] for q in range(4)], axis=0)
    sline = sline.astype(jnp.float32)
    blank = jnp.zeros((4, LANES - ZROWS - KINDS), jnp.float32)
    for j in range(16):
        table[pl.ds(j, 4, stride=16), :] = jnp.concatenate(
            [
                dline[:, ZROWS * j : ZROWS * (j + 1)],
                sline[:, KINDS * j : KINDS * (j + 1)],
                blank,
            ],
            axis=1,
        )
    for t, y in enumerate((0, 1, CELLS - 2, CELLS - 1)):
        pack[pl.ds(8 * t, 8), :] = table[pl.ds(y, 8, stride=8), :]

    pl.semaphore_wait(barrier, len(plan))
    for dx, dy, dz, tile, tiles in plan:
        if dx == 0 and dy != 0:
            first = 0 if dy > 0 else 4 - tiles
            source = pack.at[pl.ds(8 * first, 8 * tiles)]
        else:
            source = table.at[pl.ds(8 * origin(dx, tiles), 8 * tiles)]
        copy = pltpu.make_async_remote_copy(
            src_ref=source,
            dst_ref=table.at[pl.ds(8 * tile, 8 * tiles)],
            send_sem=send_a.at[0],
            recv_sem=recv_a.at[0],
            device_id=peer((dx, dy, dz), -1),
            device_id_type=pl.DeviceIdType.MESH,
        )
        copy.start()

    for copy in loads[2:]:
        copy.wait()

    pairs = nbr.shape[1]
    centre_total = cen.shape[1]
    slots = pairs // centre_total
    lane = lax.broadcasted_iota(jnp.int32, (centre_total, pairs), 1)
    row = lax.broadcasted_iota(jnp.int32, (centre_total, pairs), 0)
    mine = ((lane >= row * slots) & (lane < (row + 1) * slots)).astype(jnp.float32)
    mine16 = mine.astype(jnp.bfloat16)
    lists = jnp.concatenate(
        [cen[...], cnt[...], jnp.zeros((6, centre_total), jnp.int32)], axis=0
    ).astype(jnp.float32)
    spread = mm_exact_b(lists, mine16)
    first, count = spread[0:1], spread[1:2]
    lane1 = lax.broadcasted_iota(jnp.int32, (1, pairs), 1)
    lanef = lane1.astype(jnp.float32)
    centre_id = divided(lanef, slots)
    slot_id = lanef - centre_id * slots
    live = jnp.where(
        (slot_id < count) & (lane1 < alive[...] * slots), 1.0, 0.0
    ).astype(jnp.float32)

    cell_i = divided(first, 3.0)
    atom_i = first - 3.0 * cell_i
    col_i = divided(cell_i, CELLS)
    z_i = cell_i - CELLS * col_i
    x_i = divided(col_i, CELLS)
    y_i = col_i - CELLS * x_i

    second = nbr[...].astype(jnp.float32)
    ext = CELLS + 4
    cell_j = divided(second, 3.0)
    atom_j = second - 3.0 * cell_j
    col_j = divided(cell_j, ext)
    z_j = cell_j - ext * col_j - 2.0
    x_j = divided(col_j, ext)
    y_j = col_j - ext * x_j - 2.0
    x_j = x_j - 2.0

    def side(v):
        return jnp.where(v < 0.0, -1.0, jnp.where(v >= CELLS, 1.0, 0.0))

    sx, sy, sz = side(x_j), side(y_j), side(z_j)
    x_in, y_in, z_in = x_j - CELLS * sx, y_j - CELLS * sy, z_j - CELLS * sz
    if sizes[2] == 2:
        sz = jnp.abs(sz)
    code = sx * 9.0 + sy * 3.0 + sz
    across, along = x_in * CELLS + y_in, y_in * CELLS + x_in
    line = across
    for dx, dy, dz, tile, tiles in plan:
        if dx == 0 and dy != 0:
            value = along + float(8 * tile - 8 * origin(dy, tiles))
        else:
            value = across + float(8 * tile - 8 * origin(dx, tiles))
        line = jnp.where(code == float(dx * 9 + dy * 3 + dz), value, line)

    rows = table.shape[0]
    own = CELLS * CELLS

    def hot(index, length):
        ids = lax.broadcasted_iota(jnp.int32, (length, pairs), 0)
        return jnp.where(ids == index.astype(jnp.int32), 1.0, 0.0).astype(jnp.bfloat16)

    hot_j, hot_i = hot(line, rows), hot(col_i, own)
    lanes72 = lax.broadcasted_iota(jnp.int32, (ZROWS, pairs), 0)
    lanes24 = lax.broadcasted_iota(jnp.int32, (KINDS, pairs), 0)

    def site(atom):
        one, two = atom == 1.0, atom == 2.0
        return (
            jnp.where(one, 0.75, 0.25),
            jnp.where(one | two, 0.75, 0.25),
            jnp.where(two, 0.75, 0.25),
        )

    def picked(stack, place):
        at = place.astype(jnp.int32)
        body = stack[0:ZROWS]
        out = [
            jnp.sum(jnp.where(lanes72 == 3 * at + c, body, 0.0), axis=0, keepdims=True)
            for c in range(3)
        ]
        kind = jnp.sum(
            jnp.where(lanes24 == at, stack[ZROWS : ZROWS + KINDS], 0.0), axis=0, keepdims=True
        )
        return out, kind

    def fetch(block, onehot):
        both = raw(jnp.concatenate(halves(block.T), axis=0), onehot, NN)
        return both[:LANES] + both[LANES:]

    place_i, place_j = z_i * 3.0 + atom_i, z_in * 3.0 + atom_j
    shift_i, kind_i = picked(fetch(table[pl.ds(0, own), :], hot_i), place_i)
    site_i, site_j = site(atom_i), site(atom_j)
    two = w_two[...]
    two = jnp.concatenate([two[4:12], two[0:4], jnp.zeros_like(two[0:4])], axis=0)
    two_t, lat_t, env_t, out_t = two.T, w_lat[...].T, w_env[...].T, w_out_t[...]

    arrived = pl.ds(own, rows - own)

    def settle(ref, send, recv):
        every = pltpu.make_async_remote_copy(
            src_ref=ref.at[arrived],
            dst_ref=ref.at[arrived],
            send_sem=send.at[0],
            recv_sem=recv.at[0],
            device_id=peer(plan[0][:3], 1),
            device_id_type=pl.DeviceIdType.MESH,
        )
        every.wait()

    settle(table, send_a, recv_a)

    shift_j, kind_j = picked(fetch(table[...], hot_j), place_j)
    rx, ry, rz = [
        ((b - a) + (tb - ta) + (sb - sa)) * SIDE
        for a, b, ta, tb, sa, sb in zip(
            (x_i, y_i, z_i), (x_j, y_j, z_j), site_i, site_j, shift_i, shift_j
        )
    ]
    dist = jnp.sqrt(rx * rx + ry * ry + rz * rz)
    inv = 1.0 / dist
    ux, uy, uz = rx * inv, ry * inv, rz * inv
    ratio = dist * (1.0 / CUTOFF)
    r2 = ratio * ratio
    r5 = r2 * r2 * ratio
    inside = ratio < 1.0
    bell = jnp.where(inside, 1.0 + r5 * ratio * (-28.0 + ratio * (48.0 - 21.0 * ratio)), 0.0)
    slope = jnp.where(
        inside, r5 * (1.0 - ratio) * (1.0 - ratio) * (-168.0 / CUTOFF), 0.0
    )
    order = (lax.broadcasted_iota(jnp.int32, (NBASIS, pairs), 0) + 1).astype(jnp.float32)
    turns = order * (dist * (0.5 / CUTOFF))
    sines, cosines = wave(turns), wave(turns + 0.25)
    norm = math.sqrt(2.0 / CUTOFF)
    basis = norm * sines * (inv * bell)
    basis_d = norm * (
        cosines * order * (inv * bell * (math.pi / CUTOFF))
        + sines * (inv * (slope - bell * inv))
    )
    kinds = [1.0 - kind_i, kind_i, 1.0 - kind_j, kind_j]
    inputs = jnp.concatenate([basis] + kinds + [jnp.zeros((4, pairs), jnp.float32)], axis=0)

    hidden, hidden_d = silu_pair(mm(two_t, inputs))
    latent, latent_d = silu_pair(mm(lat_t, hidden))
    latent_h = halves(latent)
    plain = mm(env_t, latent_h)
    scale = bell * live
    weight = plain * scale
    s3, s5, s15 = math.sqrt(3.0), math.sqrt(5.0), math.sqrt(15.0)
    harm = [
        jnp.ones_like(ux),
        s3 * ux,
        s3 * uy,
        s3 * uz,
        s15 * ux * uy,
        s15 * uy * uz,
        0.5 * s5 * (3.0 * uz * uz - 1.0),
        s15 * ux * uz,
        0.5 * s15 * (ux * ux - uy * uy),
    ]
    spread_y = halves(jnp.concatenate([h * mine for h in harm], axis=0))
    weight_h = halves(weight)
    bounds = [(0, 1), (1, 4), (4, 9)]
    cuts = [slice(a * centre_total, b * centre_total) for a, b in bounds]

    def cut(pair, s):
        return pair[0][s], pair[1][s]

    environ = ENV * mm(spread_y, weight_h, NT)
    mixed = [mm(environ[s].T, cut(spread_y, s)) for s in cuts]
    width = latent.shape[0]
    joined = jnp.concatenate([latent] + [weight * a for a in mixed], axis=0)
    updated, updated_d = silu_pair(mm(out_t, joined))
    column = jnp.broadcast_to(readout[...], (8, width)).T[:, 0:1]
    score = jnp.sum(column * updated, axis=0, keepdims=True)
    pair_energy = score * scale
    energies = mm_exact_b(jnp.broadcast_to(pair_energy, (8, pairs)), mine16, NT)
    result[pl.ds(CELLS * CELLS, 8), 0:centre_total] = energies

    d_out = (column * scale) * updated_d
    back = mm(out_t.T, d_out)
    d_mixed = [back[width * (k + 1) : width * (k + 2)] for k in range(3)]
    d_weight = d_mixed[0] * mixed[0] + d_mixed[1] * mixed[1] + d_mixed[2] * mixed[2]
    passing = [halves(q * weight) for q in d_mixed]
    d_environ = ENV * jnp.concatenate(
        [mm(cut(spread_y, s), p, NT) for s, p in zip(cuts, passing)], axis=0
    )
    d_weight = d_weight + mm(d_environ.T, spread_y)
    d_spread = jnp.concatenate(
        [mm(environ[s], p) for s, p in zip(cuts, passing)], axis=0
    ) + mm(d_environ, weight_h)
    d_harm = [
        jnp.sum(
            d_spread[m * centre_total : (m + 1) * centre_total] * mine, axis=0, keepdims=True
        )
        for m in range(9)
    ]
    d_scale = score + jnp.sum(d_weight * plain, axis=0, keepdims=True)
    d_latent = back[0:width] + mm(w_env[...], d_weight * scale)
    d_hidden = mm(w_lat[...], d_latent * latent_d)
    d_inputs = mm(two, d_hidden * hidden_d)
    d_dist = (
        jnp.sum(d_inputs[0:NBASIS] * basis_d, axis=0, keepdims=True) + d_scale * live * slope
    )
    dux = s3 * d_harm[1] + s15 * (uy * d_harm[4] + uz * d_harm[7] + ux * d_harm[8])
    duy = s3 * d_harm[2] + s15 * (ux * d_harm[4] + uz * d_harm[5] - uy * d_harm[8])
    duz = s3 * d_harm[3] + s15 * (uy * d_harm[5] + ux * d_harm[7]) + 3.0 * s5 * uz * d_harm[6]
    radial = d_dist - (ux * dux + uy * duy + uz * duz) * inv
    grad = [d * inv + u * radial for d, u in ((dux, ux), (duy, uy), (duz, uz))]

    def placed(place, sign):
        at = 3 * place.astype(jnp.int32)
        out = jnp.zeros((ZROWS, pairs), jnp.float32)
        for c in range(3):
            out = jnp.where(lanes72 == at + c, sign * grad[c], out)
        return jnp.concatenate(
            [out, jnp.zeros((LANES - ZROWS, pairs), jnp.float32)], axis=0
        )

    part[...] = mm_exact_a(hot_j, placed(place_j, -1.0))
    for dx, dy, dz, tile, tiles in plan:
        copy = pltpu.make_async_remote_copy(
            src_ref=part.at[pl.ds(8 * tile, 8 * tiles)],
            dst_ref=got.at[pl.ds(8 * tile, 8 * tiles)],
            send_sem=send_b.at[0],
            recv_sem=recv_b.at[0],
            device_id=peer((dx, dy, dz), 1),
            device_id_type=pl.DeviceIdType.MESH,
        )
        copy.start()
    total[...] = part[pl.ds(0, own), :] + mm_exact_a(hot_i, placed(place_i, 1.0))
    settle(got, send_b, recv_b)
    for dx, dy, dz, tile, tiles in plan:
        if dx == 0 and dy != 0:
            for t in range(tiles):
                spot = pl.ds(origin(dy, tiles) + t, 8, stride=8)
                total[spot, :] = total[spot, :] + got[pl.ds(8 * (tile + t), 8), :]
        else:
            spot = pl.ds(8 * origin(dx, tiles), 8 * tiles)
            total[spot, :] = total[spot, :] + got[pl.ds(8 * tile, 8 * tiles), :]


def unpack_body(result, energy, forces):
    energy[0] = result[pl.ds(CELLS * CELLS, 1), 0 : energy.shape[2]]
    final = jnp.concatenate(
        [result[pl.ds(j, 4, stride=16), :][:, 0:ZROWS] for j in range(16)], axis=1
    )
    wide = 16 * ZROWS
    for q in range(4):
        forces[0, :, wide * q : wide * (q + 1)] = final[q : q + 1, :]


def solution(mesh):
    sizes = tuple(mesh.shape[a] for a in AXES)
    plan, tile_total = slot_plan(sizes[2])

    def local(displacement, species, centres, neighbours, neighbour_count, live_centres,
              w_two, w_lat, w_env, w_out, readout):
        centre_total = centres.shape[2]
        atoms = displacement.shape[2]
        vmem = pl.BlockSpec(memory_space=pltpu.VMEM)
        rows = 8 * tile_total
        args = [
            displacement, species, centres, neighbours, neighbour_count, live_centres,
            w_two, w_lat, w_env, w_out.T, readout.reshape(1, -1),
        ]

        def body(*refs):
            kernel_body(sizes, plan, *refs)

        result = pl.pallas_call(
            body,
            out_shape=jax.ShapeDtypeStruct((CELLS * CELLS + 8, LANES), jnp.float32),
            in_specs=[pl.BlockSpec(memory_space=pltpu.HBM)] * len(args),
            out_specs=vmem,
            scratch_shapes=[pltpu.VMEM(x.shape, x.dtype) for x in args]
            + [
                pltpu.VMEM((rows, LANES), jnp.float32),
                pltpu.VMEM((32, LANES), jnp.float32),
                pltpu.VMEM((rows, LANES), jnp.float32),
                pltpu.VMEM((rows, LANES), jnp.float32),
            ]
            + [pltpu.SemaphoreType.DMA((1,))] * 4
            + [pltpu.SemaphoreType.DMA((len(args),))],
            compiler_params=pltpu.CompilerParams(collective_id=0, has_side_effects=True),
        )(*args)
        return pl.pallas_call(
            unpack_body,
            out_shape=(
                jax.ShapeDtypeStruct(centres.shape, jnp.float32),
                jax.ShapeDtypeStruct(displacement.shape, jnp.float32),
            ),
            in_specs=[vmem],
            out_specs=(vmem, vmem),
        )(result)

    split = P(*AXES)
    return jax.shard_map(
        local,
        mesh=mesh,
        in_specs=(split,) * 6 + (P(),) * 5,
        out_specs=(split, split),
        check_vma=False,
    )
```

profile of v0, /device:TPU:0, one launch (start us, length us, event | category | flops | bytes accessed | tf_op | source)
XLA Modules:
  0.0 24.1 jit_solution(10127456745397200437)
XLA Ops:
  1.3 21.4 %shard_map.122.result = f32[72,128]{1,0:T(8,128)} custom-call(f32[1,1,4608]{2,1,0:T(1,128)} %refs_0_.1, s32[1,1,1536]{2,1,0:T(1,128)} %refs_1_.1, s32[1,1,16]{2,1,0:T(1,128)} %refs_2_.1, s32[1,1,512]{2,1,0:T(1,128)} %refs_3_.1, s32[1,1,16]{2,1,0:T(1,128)} %refs_4_.1, s32[1,1,1]{2,1,0:T(1,128)S(6)} %copy.13.refs_5_, f32[12,64]{1,0:T(8,128)} %refs_6_.1, ...), custom_call_target="tpu_custom_call" | custom-call | tf_op jit(solution)/shard_map/pallas_call | solution.py:451
  22.6 1.5 %shard_map.123 = (f32[1,1,16]{2,1,0:T(1,128)}, f32[1,1,4608]{2,1,0:T(1,128)}) custom-call(f32[72,128]{1,0:T(8,128)} %shard_map.122.result), custom_call_target="tpu_custom_call" | custom-call | tf_op jit(solution)/shard_map/pallas_call | solution.py:467
where the time goes:
time: 24.3 us; the launch traced here: 24.1 us
  Pallas kernels  22.8 us (94%)
  between operations  1.29 us (5%)
    pallas_call x1, Pallas kernels, local(): pl.pallas_call(body, out_shape=jax.ShapeDtypeStruct((CELLS * CELLS + 8, L...  21.4 us
    pallas_call x1, Pallas kernels, local(): pl.pallas_call(unpack_body, out_shape=(jax.ShapeDtypeStruct(centres.shape...  1.47 us

commit v1 on v0

v1 whole, which is shorter than its diff:
```python
import math

import jax
import jax.numpy as jnp
from jax import lax
from jax.experimental import pallas as pl
from jax.experimental.pallas import tpu as pltpu
from jax.sharding import PartitionSpec as P

CELLS = 8
NBASIS = 8
CUTOFF = 6.0
SIDE = 3.1
ENV = 0.2
LANES = 128
ZROWS = CELLS * 9
KINDS = CELLS * 3
KEPT = 18
KIND_AT = ZROWS + KEPT
HALF = CELLS * CELLS // 2
AXES = ("gx", "gy", "gz")

NN = (((1,), (0,)), ((), ()))
NT = (((1,), (1,)), ((), ()))


def halves(x):
    hi = x.astype(jnp.bfloat16)
    lo = (x - hi.astype(jnp.float32)).astype(jnp.bfloat16)
    return hi, lo


def raw(a, b, dims):
    return lax.dot_general(a, b, dims, preferred_element_type=jnp.float32)


def mm(a, b, dims=NN):
    ah, al = a if isinstance(a, tuple) else halves(a)
    bh, bl = b if isinstance(b, tuple) else halves(b)
    if dims is NT:
        m, n = ah.shape[0], bh.shape[0]
        both = raw(jnp.concatenate([ah, al], axis=0), jnp.concatenate([bh, bl], axis=0), NT)
        return both[:m, :n] + (both[:m, n:] + both[m:, :n])
    if ah.shape[1] > 2 * LANES - 1:
        return raw(ah, bh, dims) + (raw(ah, bl, dims) + raw(al, bh, dims))
    return raw(
        jnp.concatenate([ah, ah, al], axis=1), jnp.concatenate([bh, bl, bh], axis=0), NN
    )


def mm_exact_b(a, b, dims=NN):
    ah, al = halves(a)
    return raw(ah, b, dims) + raw(al, b, dims)


def mm_exact_a(a, b):
    n = b.shape[0]
    both = raw(a, jnp.concatenate(halves(b), axis=0), NT)
    return both[:, :n] + both[:, n:]


def slot_plan(depth):
    sides = [1] if depth == 2 else [1, -1]
    ends = (-1, 1)
    groups = [
        [((0, 0, dz), HALF) for dz in sides],
        [((dx, 0, 0), 2 * CELLS) for dx in ends],
        [((0, dy, 0), 2 * CELLS) for dy in ends],
        [((dx, 0, dz), CELLS) for dz in sides for dx in ends],
        [((0, dy, dz), CELLS // 2) for dz in sides for dy in ends],
        [((dx, dy, 0), 1) for dx in ends for dy in ends],
        [((dx, dy, dz), 1) for dz in sides for dx in ends for dy in ends],
    ]
    plan, at = [], 0
    for step, rows in [entry for group in groups for entry in group]:
        plan.append((step, at, rows))
        at += rows
    return plan, at


def origin(step, tiles):
    return 0 if step >= 0 else CELLS - tiles


def own_corner(step):
    return step[2] == 0 and step[0] != 0 and step[1] != 0


def wave(turns):
    f = turns - jnp.floor(turns + 0.5)
    f = jnp.where(f > 0.25, 0.5 - f, jnp.where(f < -0.25, -0.5 - f, f))
    x = f * (2.0 * math.pi)
    s = x * x
    p = -1.0 / 39916800.0
    for c in (1.0 / 362880.0, -1.0 / 5040.0, 1.0 / 120.0, -1.0 / 6.0):
        p = p * s + c
    return x + x * s * p


def divided(value, by):
    return jnp.floor((value + 0.5) * (1.0 / by))


def silu_pair(x):
    s = 1.0 / (1.0 + jnp.exp(-x))
    return x * s, s * (1.0 + x * (1.0 - s))


def kernel_body(sizes, plan, disp_hbm, spec_hbm, cen_hbm, nbr_hbm, cnt_hbm, alive_hbm, two_hbm,
                lat_hbm, env_hbm, out_hbm, readout_hbm, result,
                disp, spec, cen, nbr, cnt, alive, w_two, w_lat, w_env, w_out_t, readout,
                table, pack, ztable, zpack, mail, inbox, back_mail, back_inbox, halo, part, got,
                send_a, recv_a, send_b, recv_b, load):
    loads = [
        pltpu.make_async_copy(src, dst, load.at[at])
        for at, (src, dst) in enumerate(
            (
                (disp_hbm, disp),
                (spec_hbm, spec),
                (cen_hbm, cen),
                (nbr_hbm, nbr),
                (cnt_hbm, cnt),
                (alive_hbm, alive),
                (two_hbm, w_two),
                (lat_hbm, w_lat),
                (env_hbm, w_env),
                (out_hbm, w_out_t),
                (readout_hbm, readout),
            )
        )
    ]
    for copy in loads:
        copy.start()
    disp, spec, cen, nbr, cnt, alive = (
        ref.at[0] for ref in (disp, spec, cen, nbr, cnt, alive)
    )
    total = result.at[pl.ds(0, CELLS * CELLS)]
    me = tuple(lax.axis_index(a) for a in AXES)
    odd = [lax.rem(i, 2) for i in me[:2]]
    swapped = tuple(i + 1 - 2 * o for i, o in zip(me, odd)) + me[2:]

    def moved(place, step, sign):
        return tuple(
            lax.rem(i + (sign * d + n), n) if d else i for i, d, n in zip(place, step, sizes)
        )

    def holder(step):
        return moved(swapped, step, 1)

    def worker(step):
        x, y, z = moved(me, step, -1)
        return x + 1 - 2 * lax.rem(x, 2), y + 1 - 2 * lax.rem(y, 2), z

    def mine_too(step):
        return (odd[0] == (1 if step[0] > 0 else 0)) & (odd[1] == (1 if step[1] > 0 else 0))

    barrier = pltpu.get_barrier_semaphore()

    def greet(device):
        pl.semaphore_signal(
            barrier, inc=1, device_id=device, device_id_type=pl.DeviceIdType.MESH
        )

    def unless_mine(step, action):
        if own_corner(step):
            pl.when(jnp.logical_not(mine_too(step)))(action)
        else:
            action()

    for step, at, rows in reversed(plan):
        unless_mine(step, lambda step=step: greet(holder(step)))
    greet(swapped)

    for copy in loads[:2]:
        copy.wait()
    dwide, swide = 16 * ZROWS, 16 * KINDS
    dline = jnp.concatenate([disp[:, dwide * q : dwide * (q + 1)] for q in range(4)], axis=0)
    sline = jnp.concatenate([spec[:, swide * q : swide * (q + 1)] for q in range(4)], axis=0)
    sline = sline.astype(jnp.float32)
    gap = jnp.zeros((4, KEPT), jnp.float32)
    blank = jnp.zeros((4, LANES - KIND_AT - KINDS), jnp.float32)
    for j in range(16):
        kinds = sline[:, KINDS * j : KINDS * (j + 1)]
        table[pl.ds(j, 4, stride=16), :] = jnp.concatenate(
            [
                dline[:, ZROWS * j : ZROWS * (j + 1)],
                gap,
                kinds[:, KINDS - 6 : KINDS],
                kinds[:, 0 : KINDS - 6],
                blank,
            ],
            axis=1,
        )
    lane_row = lax.broadcasted_iota(jnp.int32, (1, LANES), 1)

    def high(shape):
        ids = lax.broadcasted_iota(jnp.int32, shape, 1)
        return (
            ((ids >= KEPT) & (ids < 2 * KEPT))
            | ((ids >= ZROWS) & (ids < KIND_AT))
            | ((ids >= KIND_AT + KEPT) & (ids < KIND_AT + KEPT + 12))
        )

    ztable[...] = jnp.where(
        high((HALF, LANES)),
        pltpu.roll(table[pl.ds(HALF, HALF), :], KEPT, 1),
        table[pl.ds(0, HALF), :],
    )
    for t, y in enumerate((0, 1, CELLS - 2, CELLS - 1)):
        pack[pl.ds(8 * t, 8), :] = table[pl.ds(y, 8, stride=8), :]
    for t, y in enumerate((0, CELLS - 1)):
        zpack[pl.ds(4 * t, 4), :] = ztable[pl.ds(y, 4, stride=8), :]

    def source(step, rows):
        dx, dy, dz = step
        if dx and dy:
            if dz:
                return ztable.at[pl.ds((HALF - CELLS) * (dx < 0) + (CELLS - 1) * (dy < 0), 1)]
            return table.at[pl.ds(CELLS * (CELLS - 1) * (dx < 0) + (CELLS - 1) * (dy < 0), 1)]
        if dy:
            return (zpack if dz else pack).at[pl.ds(0 if dy > 0 else rows, rows)]
        if dz:
            return ztable.at[pl.ds(HALF - rows if dx < 0 else 0, rows)]
        return table.at[pl.ds(CELLS * origin(dx, 2), rows)]

    def remote(src, dst, send, recv, device):
        return pltpu.make_async_remote_copy(
            src_ref=src,
            dst_ref=dst,
            send_sem=send,
            recv_sem=recv,
            device_id=device,
            device_id_type=pl.DeviceIdType.MESH,
        )

    pl.semaphore_wait(barrier, len(plan))
    for step, at, rows in reversed(plan):
        copy = remote(
            source(step, rows), halo.at[pl.ds(at, rows)], send_a.at[0], recv_a.at[0], worker(step)
        )
        unless_mine(step, copy.start)

    for copy in loads[2:]:
        copy.wait()

    pairs = nbr.shape[1]
    centre_total = cen.shape[1]
    slots = pairs // centre_total
    lane = lax.broadcasted_iota(jnp.int32, (centre_total, pairs), 1)
    row = lax.broadcasted_iota(jnp.int32, (centre_total, pairs), 0)
    mine = ((lane >= row * slots) & (lane < (row + 1) * slots)).astype(jnp.float32)
    mine16 = mine.astype(jnp.bfloat16)
    own = CELLS * CELLS

    def site(atom):
        one, two = atom == 1.0, atom == 2.0
        return (
            jnp.where(one, 0.75, 0.25),
            jnp.where(one | two, 0.75, 0.25),
            jnp.where(two, 0.75, 0.25),
        )

    def kind_lane(z, atom):
        turned = jnp.where(z >= CELLS - 2, z - (CELLS - 2), z + 2.0)
        return KIND_AT + 3.0 * turned + atom

    first = cen[...].astype(jnp.float32)
    cell_i = divided(first, 3.0)
    atom_i = first - 3.0 * cell_i
    col_i = divided(cell_i, CELLS)
    z_i = cell_i - CELLS * col_i
    x_i = divided(col_i, CELLS)
    y_i = col_i - CELLS * x_i
    spot_i = [a + b for a, b in zip((x_i, y_i, z_i), site(atom_i))]
    alive_lane = lax.broadcasted_iota(jnp.int32, (1, centre_total), 1)
    count = jnp.where(alive_lane < alive[...], cnt[...], 0).astype(jnp.float32)
    spread = raw(
        jnp.concatenate(
            spot_i + [count, jnp.zeros((4, centre_total), jnp.float32)], axis=0
        ).astype(jnp.bfloat16),
        mine16,
        NN,
    )
    lanef = lax.broadcasted_iota(jnp.int32, (1, pairs), 1).astype(jnp.float32)
    slot_id = lanef - slots * divided(lanef, slots)
    live = jnp.where(slot_id < spread[3:4], 1.0, 0.0).astype(jnp.float32)

    second = nbr[...].astype(jnp.float32)
    ext = CELLS + 4
    cell_j = divided(second, 3.0)
    atom_j = second - 3.0 * cell_j
    col_j = divided(cell_j, ext)
    z_j = cell_j - ext * col_j - 2.0
    x_j = divided(col_j, ext)
    y_j = col_j - ext * x_j - 2.0
    x_j = x_j - 2.0

    def side(v):
        return jnp.where(v < 0.0, -1.0, jnp.where(v >= CELLS, 1.0, 0.0))

    sx, sy, sz = side(x_j), side(y_j), side(z_j)
    x_in, y_in, z_in = x_j - CELLS * sx, y_j - CELLS * sy, z_j - CELLS * sz
    if sizes[2] == 2:
        sz = jnp.abs(sz)
    code = sx * 9.0 + sy * 3.0 + sz
    upper = jnp.where(x_in >= CELLS // 2, 1.0, 0.0)
    across, along = x_in * CELLS + y_in, y_in * CELLS + x_in
    line = jnp.full_like(code, -1.0)
    for (dx, dy, dz), at, rows in plan:
        if dx and dy:
            value = float(at)
        elif dz and dy:
            value = x_in - (CELLS // 2) * upper + float(at)
        elif dz and dx:
            value = y_in + float(at)
        elif dz:
            value = across - HALF * upper + float(at)
        elif dy:
            value = along + float(at - CELLS * origin(dy, 2))
        else:
            value = across + float(at - CELLS * origin(dx, 2))
        line = jnp.where(code == float(dx * 9 + dy * 3 + dz), value, line)
    raised = jnp.where(sz != 0.0, KEPT * upper, 0.0)
    place_j = 9.0 * z_in + 3.0 * atom_j + raised
    kind_at_j = kind_lane(z_in, atom_j) + raised
    inner = jnp.where(code == 0.0, across, -1.0)

    tail = jnp.full((1, LANES - centre_total), -8.0, jnp.float32)
    column = jnp.concatenate([inner, col_i, tail], axis=1).astype(jnp.int32)
    place = jnp.concatenate(
        [jnp.where(code == 0.0, place_j, -8.0), 9.0 * z_i + 3.0 * atom_i, tail], axis=1
    ).astype(jnp.int32)
    kind_at = jnp.concatenate([kind_at_j, kind_lane(z_i, atom_i), tail], axis=1).astype(jnp.int32)

    def hot(index, length):
        ids = lax.broadcasted_iota(jnp.int32, (length, index.shape[1]), 0)
        return jnp.where(ids == index, 1.0, 0.0).astype(jnp.bfloat16)

    def picked(stack, at, kind_at):
        ids = lax.broadcasted_iota(jnp.int32, stack.shape, 0)
        body, body_ids = stack[0:96], ids[0:96]
        out = [
            jnp.sum(jnp.where(body_ids == at + c, body, 0.0), axis=0, keepdims=True)
            for c in range(3)
        ]
        kind = jnp.sum(
            jnp.where(ids[88:120] == kind_at, stack[88:120], 0.0), axis=0, keepdims=True
        )
        return out, kind

    def fetch(block, onehot):
        both = raw(jnp.concatenate(halves(block.T), axis=0), onehot, NN)
        return both[:LANES] + both[LANES:]

    hot_own = hot(column, own)
    shift, kind = picked(fetch(table[...], hot_own), place, kind_at)
    from_centre = mm_exact_b(
        jnp.concatenate(
            [v[:, pairs : pairs + centre_total] for v in shift + [kind]]
            + [jnp.zeros((4, centre_total), jnp.float32)],
            axis=0,
        ),
        mine16,
    )
    spot_j = [a + b for a, b in zip((x_j, y_j, z_j), site(atom_j))]
    mail[...] = jnp.concatenate(
        [
            ((spot_j[c] - spread[c : c + 1]) + (shift[c][:, 0:pairs] - from_centre[c : c + 1]))
            * SIDE
            for c in range(3)
        ]
        + [
            from_centre[3:4] + 2.0 * live,
            jnp.where(code == 0.0, kind[:, 0:pairs], 0.0),
            line,
            place_j,
            kind_at_j,
        ],
        axis=0,
    )
    post = remote(mail, inbox, send_a.at[1], recv_a.at[1], worker((0, 0, 0)))
    post.start()

    two = w_two[...]
    two = jnp.concatenate([two[4:12], two[0:4], jnp.zeros_like(two[0:4])], axis=0)
    two_t, lat_t, env_t, out_t = two.T, w_lat[...].T, w_env[...].T, w_out_t[...]

    crossing = plan[-1][1] + plan[-1][2] - 1
    halo_rows = halo.shape[0]

    def every(ref, send, recv):
        span = pl.ds(0, crossing)
        return remote(ref.at[span], ref.at[span], send, recv, swapped)

    post.wait_recv()
    arrivals = every(halo, send_a.at[0], recv_a.at[0])
    arrivals.wait_recv()

    ids = lax.broadcasted_iota(jnp.int32, (8, LANES), 0)

    def with_mine(block, row_of):
        pieces = block
        corner = [(step, at) for step, at, rows in plan if own_corner(step)]
        base = corner[0][1] // 8 * 8
        tile = block[base : base + 8]
        for step, at in corner:
            tile = jnp.where((ids == at - base) & mine_too(step), row_of(step, at), tile)
        pieces = [block[0:base], tile, block[base + 8 :]]
        return jnp.concatenate([p for p in pieces if p.shape[0]], axis=0)

    letter = inbox[...]
    block = with_mine(halo[...], lambda step, at: source(step, 1)[...])
    total_rows = plan[-1][1] + plan[-1][2]
    if total_rows < halo_rows:
        every_id = lax.broadcasted_iota(jnp.int32, (halo_rows, LANES), 0)
        block = jnp.where(every_id < total_rows, block, 0.0)
    hot_j = hot(letter[5:6].astype(jnp.int32), halo_rows)
    there = letter[6:7].astype(jnp.int32)
    shift_j, kind_j = picked(fetch(block, hot_j), there, letter[7:8].astype(jnp.int32))
    rx, ry, rz = [letter[c : c + 1] + SIDE * shift_j[c] for c in range(3)]
    live = jnp.where(letter[3:4] > 1.5, 1.0, 0.0)
    kind_i = letter[3:4] - 2.0 * live
    kind_j = letter[4:5] + kind_j
    dist = jnp.sqrt(rx * rx + ry * ry + rz * rz)
    inv = 1.0 / dist
    ux, uy, uz = rx * inv, ry * inv, rz * inv
    ratio = dist * (1.0 / CUTOFF)
    r2 = ratio * ratio
    r5 = r2 * r2 * ratio
    inside = ratio < 1.0
    bell = jnp.where(inside, 1.0 + r5 * ratio * (-28.0 + ratio * (48.0 - 21.0 * ratio)), 0.0)
    slope = jnp.where(
        inside, r5 * (1.0 - ratio) * (1.0 - ratio) * (-168.0 / CUTOFF), 0.0
    )
    order = (lax.broadcasted_iota(jnp.int32, (NBASIS, pairs), 0) + 1).astype(jnp.float32)
    turns = order * (dist * (0.5 / CUTOFF))
    sines, cosines = wave(turns), wave(turns + 0.25)
    norm = math.sqrt(2.0 / CUTOFF)
    basis = norm * sines * (inv * bell)
    basis_d = norm * (
        cosines * order * (inv * bell * (math.pi / CUTOFF))
        + sines * (inv * (slope - bell * inv))
    )
    kinds = [1.0 - kind_i, kind_i, 1.0 - kind_j, kind_j]
    inputs = jnp.concatenate([basis] + kinds + [jnp.zeros((4, pairs), jnp.float32)], axis=0)

    hidden, hidden_d = silu_pair(mm(two_t, inputs))
    latent, latent_d = silu_pair(mm(lat_t, hidden))
    latent_h = halves(latent)
    plain = mm(env_t, latent_h)
    scale = bell * live
    weight = plain * scale
    s3, s5, s15 = math.sqrt(3.0), math.sqrt(5.0), math.sqrt(15.0)
    harm = [
        jnp.ones_like(ux),
        s3 * ux,
        s3 * uy,
        s3 * uz,
        s15 * ux * uy,
        s15 * uy * uz,
        0.5 * s5 * (3.0 * uz * uz - 1.0),
        s15 * ux * uz,
        0.5 * s15 * (ux * ux - uy * uy),
    ]
    spread_y = halves(jnp.concatenate([h * mine for h in harm], axis=0))
    weight_h = halves(weight)
    bounds = [(0, 1), (1, 4), (4, 9)]
    cuts = [slice(a * centre_total, b * centre_total) for a, b in bounds]

    def cut(pair, s):
        return pair[0][s], pair[1][s]

    environ = ENV * mm(spread_y, weight_h, NT)
    mixed = [mm(environ[s].T, cut(spread_y, s)) for s in cuts]
    width = latent.shape[0]
    joined = jnp.concatenate([latent] + [weight * a for a in mixed], axis=0)
    updated, updated_d = silu_pair(mm(out_t, joined))
    gain = jnp.broadcast_to(readout[...], (8, width)).T[:, 0:1]
    score = jnp.sum(gain * updated, axis=0, keepdims=True)
    pair_energy = score * scale

    d_out = (gain * scale) * updated_d
    back = mm(out_t.T, d_out)
    d_mixed = [back[width * (k + 1) : width * (k + 2)] for k in range(3)]
    d_weight = d_mixed[0] * mixed[0] + d_mixed[1] * mixed[1] + d_mixed[2] * mixed[2]
    passing = [halves(q * weight) for q in d_mixed]
    d_environ = ENV * jnp.concatenate(
        [mm(cut(spread_y, s), p, NT) for s, p in zip(cuts, passing)], axis=0
    )
    d_weight = d_weight + mm(d_environ.T, spread_y)
    d_spread = jnp.concatenate(
        [mm(environ[s], p) for s, p in zip(cuts, passing)], axis=0
    ) + mm(d_environ, weight_h)
    d_harm = [
        jnp.sum(
            d_spread[m * centre_total : (m + 1) * centre_total] * mine, axis=0, keepdims=True
        )
        for m in range(9)
    ]
    d_scale = score + jnp.sum(d_weight * plain, axis=0, keepdims=True)
    d_latent = back[0:width] + mm(w_env[...], d_weight * scale)
    d_hidden = mm(w_lat[...], d_latent * latent_d)
    d_inputs = mm(two, d_hidden * hidden_d)
    d_dist = (
        jnp.sum(d_inputs[0:NBASIS] * basis_d, axis=0, keepdims=True) + d_scale * live * slope
    )
    dux = s3 * d_harm[1] + s15 * (uy * d_harm[4] + uz * d_harm[7] + ux * d_harm[8])
    duy = s3 * d_harm[2] + s15 * (ux * d_harm[4] + uz * d_harm[5] - uy * d_harm[8])
    duz = s3 * d_harm[3] + s15 * (uy * d_harm[5] + ux * d_harm[7]) + 3.0 * s5 * uz * d_harm[6]
    radial = d_dist - (ux * dux + uy * duy + uz * duz) * inv
    grad = [d * inv + u * radial for d, u in ((dux, ux), (duy, uy), (duz, uz))]


    back_mail[0:3, 0:pairs] = jnp.concatenate(grad, axis=0)
    sums = mm_exact_b(
        jnp.concatenate(grad + [pair_energy, jnp.zeros((4, pairs), jnp.float32)], axis=0),
        mine16,
        NT,
    )
    back_mail[:, pairs : pairs + centre_total] = sums[0:4]
    reply = remote(back_mail, back_inbox, send_b.at[1], recv_b.at[1], swapped)
    reply.start()

    def placed(at, values):
        ids = lax.broadcasted_iota(jnp.int32, (96, at.shape[1]), 0)
        out = jnp.zeros(ids.shape, jnp.float32)
        for c in range(3):
            out = jnp.where(ids == at + c, values[c], out)
        return jnp.concatenate(
            [out, jnp.zeros((LANES - 96, at.shape[1]), jnp.float32)], axis=0
        )

    part[...] = mm_exact_a(hot_j, placed(there, [-g for g in grad]))
    for step, at, rows in reversed(plan):
        span = pl.ds(at, rows)
        copy = remote(part.at[span], got.at[span], send_b.at[0], recv_b.at[0], holder(step))
        unless_mine(step, copy.start)

    reply.wait_recv()
    answer = back_inbox[...]
    signs = jnp.where(
        lax.broadcasted_iota(jnp.int32, (1, pairs + LANES), 1) < pairs, -1.0, 1.0
    )
    total[...] = mm_exact_a(
        hot_own, placed(place, [signs * answer[c : c + 1] for c in range(3)])
    )
    result[pl.ds(own, 8), 0:centre_total] = jnp.broadcast_to(
        answer[3:4, pairs : pairs + centre_total], (8, centre_total)
    )
    returns = every(got, send_b.at[0], recv_b.at[0])
    returns.wait_recv()

    def add(spot, value):
        total[spot, :] = total[spot, :] + value

    for (dx, dy, dz), at, rows in plan:
        value = got[pl.ds(at, rows), :]
        x, y = (CELLS - 1) * (dx < 0), (CELLS - 1) * (dy < 0)
        if own_corner((dx, dy, dz)):
            value = jnp.where(mine_too((dx, dy, dz)), part[pl.ds(at, 1), :], value)
            add(pl.ds(CELLS * x + y, 1), value)
        elif dz:
            top = high(value.shape)
            low = jnp.where(top, 0.0, value)
            lifted = pltpu.roll(jnp.where(top, value, 0.0), LANES - KEPT, 1)
            if dx:
                spot = pl.ds(CELLS * x + y, rows)
                add(spot, lifted if dx < 0 else low)
            elif dy:
                add(pl.ds(y, rows, stride=CELLS), low)
                add(pl.ds(HALF + y, rows, stride=CELLS), lifted)
            else:
                add(pl.ds(0, HALF), low)
                add(pl.ds(HALF, HALF), lifted)
        elif dy:
            for t in range(2):
                add(pl.ds(origin(dy, 2) + t, 8, stride=8), value[8 * t : 8 * t + 8])
        else:
            add(pl.ds(CELLS * origin(dx, 2), rows), value)
    for copy in (post, arrivals, reply, returns):
        copy.wait_send()


def unpack_body(result, energy, forces):
    energy[0] = result[pl.ds(CELLS * CELLS, 1), 0 : energy.shape[2]]
    final = jnp.concatenate(
        [result[pl.ds(j, 4, stride=16), :][:, 0:ZROWS] for j in range(16)], axis=1
    )
    wide = 16 * ZROWS
    for q in range(4):
        forces[0, :, wide * q : wide * (q + 1)] = final[q : q + 1, :]


def solution(mesh):
    sizes = tuple(mesh.shape[a] for a in AXES)
    plan, line_total = slot_plan(sizes[2])

    def local(displacement, species, centres, neighbours, neighbour_count, live_centres,
              w_two, w_lat, w_env, w_out, readout):
        pairs = neighbours.shape[2]
        vmem = pl.BlockSpec(memory_space=pltpu.VMEM)
        rows = -(-line_total // 8) * 8
        args = [
            displacement, species, centres, neighbours, neighbour_count, live_centres,
            w_two, w_lat, w_env, w_out.T, readout.reshape(1, -1),
        ]

        def body(*refs):
            kernel_body(sizes, plan, *refs)

        sizes_vmem = [
            (CELLS * CELLS, LANES), (4 * CELLS, LANES), (HALF, LANES), (CELLS, LANES),
            (8, pairs), (8, pairs), (4, pairs + LANES), (4, pairs + LANES),
            (rows, LANES), (rows, LANES), (rows, LANES),
        ]
        result = pl.pallas_call(
            body,
            out_shape=jax.ShapeDtypeStruct((CELLS * CELLS + 8, LANES), jnp.float32),
            in_specs=[pl.BlockSpec(memory_space=pltpu.HBM)] * len(args),
            out_specs=vmem,
            scratch_shapes=[pltpu.VMEM(x.shape, x.dtype) for x in args]
            + [pltpu.VMEM(shape, jnp.float32) for shape in sizes_vmem]
            + [pltpu.SemaphoreType.DMA((2,))] * 4
            + [pltpu.SemaphoreType.DMA((len(args),))],
            compiler_params=pltpu.CompilerParams(collective_id=0, has_side_effects=True),
        )(*args)
        return pl.pallas_call(
            unpack_body,
            out_shape=(
                jax.ShapeDtypeStruct(centres.shape, jnp.float32),
                jax.ShapeDtypeStruct(displacement.shape, jnp.float32),
            ),
            in_specs=[vmem],
            out_specs=(vmem, vmem),
        )(result)

    split = P(*AXES)
    return jax.shard_map(
        local,
        mesh=mesh,
        in_specs=(split,) * 6 + (P(),) * 5,
        out_specs=(split, split),
        check_vma=False,
    )
```

time: 24.3 us -> 20.3 us (0.84)
  Pallas kernels: 22.8 us -> 18.8 us
    pallas_call x1, Pallas kernels: 21.4 us -> 17.3 us  [local(): pl.pallas_call(body, out_shape=jax.ShapeDtypeStruct((CELLS * CELLS + 8, L...]
where the time goes in v1:
time: 20.3 us; the launch traced here: 20.1 us
  Pallas kernels  18.8 us (93%)
  between operations  1.29 us (6%)
    pallas_call x1, Pallas kernels, local(): pl.pallas_call(body, out_shape=jax.ShapeDtypeStruct((CELLS * CELLS + 8, L...  17.3 us
    pallas_call x1, Pallas kernels, local(): pl.pallas_call(unpack_body, out_shape=(jax.ShapeDtypeStruct(centres.shape...  1.47 us

profile of v1, /device:TPU:0, one launch (start us, length us, event | category | flops | bytes accessed | tf_op | source)
XLA Modules:
  0.0 20.1 jit_solution(7816898359907181066)
XLA Ops:
  1.3 17.3 %shard_map.122.result = f32[72,128]{1,0:T(8,128)} custom-call(f32[1,1,4608]{2,1,0:T(1,128)} %refs_0_.1, s32[1,1,1536]{2,1,0:T(1,128)} %refs_1_.1, s32[1,1,16]{2,1,0:T(1,128)} %refs_2_.1, s32[1,1,512]{2,1,0:T(1,128)} %refs_3_.1, s32[1,1,16]{2,1,0:T(1,128)} %refs_4_.1, s32[1,1,1]{2,1,0:T(1,128)S(6)} %copy.13.refs_5_, f32[12,64]{1,0:T(8,128)} %refs_6_.1, ...), custom_call_target="tpu_custom_call" | custom-call | tf_op jit(solution)/shard_map/pallas_call | solution.py:616
  18.6 1.5 %shard_map.123 = (f32[1,1,16]{2,1,0:T(1,128)}, f32[1,1,4608]{2,1,0:T(1,128)}) custom-call(f32[72,128]{1,0:T(8,128)} %shard_map.122.result), custom_call_target="tpu_custom_call" | custom-call | tf_op jit(solution)/shard_map/pallas_call | solution.py:627

commit v2 on v1

--- a/solution.py
+++ b/solution.py
@@ -615,7 +615,7 @@
         ]
         result = pl.pallas_call(
             body,
-            out_shape=jax.ShapeDtypeStruct((CELLS * CELLS + 8, LANES), jnp.float32),
+            out_shape=pltpu.VMEM((CELLS * CELLS + 8, LANES), jnp.float32),
             in_specs=[pl.BlockSpec(memory_space=pltpu.HBM)] * len(args),
             out_specs=vmem,
             scratch_shapes=[pltpu.VMEM(x.shape, x.dtype) for x in args]
@@ -624,6 +624,7 @@
             + [pltpu.SemaphoreType.DMA((len(args),))],
             compiler_params=pltpu.CompilerParams(collective_id=0, has_side_effects=True),
         )(*args)
+        result = pltpu.with_memory_space_constraint(result, pltpu.VMEM)
         return pl.pallas_call(
             unpack_body,
             out_shape=(

time: 20.3 us -> 18.8 us (0.926)
  Pallas kernels: 18.8 us -> 17.4 us
    pallas_call x1, Pallas kernels: 1.47 us -> 0.7 us  [local(): pl.pallas_call(unpack_body, out_shape=(jax.ShapeDtypeStruct(centres.shape...]
    pallas_call x1, Pallas kernels: 17.3 us -> 16.7 us  [local(): pl.pallas_call(body, out_shape=pltpu.VMEM((CELLS * CELLS + 8, LANES), jnp...]
where the time goes in v2:
time: 18.8 us; the launch traced here: 18.7 us
  Pallas kernels  17.4 us (93%)
  between operations  1.29 us (7%)
    pallas_call x1, Pallas kernels, local(): pl.pallas_call(body, out_shape=pltpu.VMEM((CELLS * CELLS + 8, LANES), jnp...  16.7 us
    pallas_call x1, Pallas kernels, local(): pl.pallas_call(unpack_body, out_shape=(jax.ShapeDtypeStruct(centres.shape...  0.7 us

profile of v2, /device:TPU:0, one launch (start us, length us, event | category | flops | bytes accessed | tf_op | source)
XLA Modules:
  0.0 18.7 jit_solution(15308160973657947851)
XLA Ops:
  1.3 16.7 %shard_map.122.result = f32[72,128]{1,0:T(8,128)S(1)} custom-call(f32[1,1,4608]{2,1,0:T(1,128)} %refs_0_.1, s32[1,1,1536]{2,1,0:T(1,128)} %refs_1_.1, s32[1,1,16]{2,1,0:T(1,128)} %refs_2_.1, s32[1,1,512]{2,1,0:T(1,128)} %refs_3_.1, s32[1,1,16]{2,1,0:T(1,128)} %refs_4_.1, s32[1,1,1]{2,1,0:T(1,128)S(6)} %copy.13.refs_5_, f32[12,64]{1,0:T(8,128)} %refs_6_.1, ...), custom_call_target="tpu_custom_call" | custom-call | tf_op jit(solution)/shard_map/pallas_call | solution.py:616
  18.0 0.7 %shard_map.123 = (f32[1,1,16]{2,1,0:T(1,128)}, f32[1,1,4608]{2,1,0:T(1,128)}) custom-call(f32[72,128]{1,0:T(8,128)S(1)} %shard_map.122.result), custom_call_target="tpu_custom_call" | custom-call | tf_op jit(solution)/shard_map/pallas_call | solution.py:628

commit v3 on v2

--- a/solution.py
+++ b/solution.py
@@ -34,18 +34,24 @@
     return lax.dot_general(a, b, dims, preferred_element_type=jnp.float32)
 
 
-def mm(a, b, dims=NN):
-    ah, al = a if isinstance(a, tuple) else halves(a)
-    bh, bl = b if isinstance(b, tuple) else halves(b)
-    if dims is NT:
-        m, n = ah.shape[0], bh.shape[0]
-        both = raw(jnp.concatenate([ah, al], axis=0), jnp.concatenate([bh, bl], axis=0), NT)
-        return both[:m, :n] + (both[:m, n:] + both[m:, :n])
-    if ah.shape[1] > 2 * LANES - 1:
-        return raw(ah, bh, dims) + (raw(ah, bl, dims) + raw(al, bh, dims))
-    return raw(
-        jnp.concatenate([ah, ah, al], axis=1), jnp.concatenate([bh, bl, bh], axis=0), NN
-    )
+def thrice(a):
+    high, low = halves(a)
+    return jnp.concatenate([high, high, low], axis=1)
+
+
+def stacked(b):
+    high, low = halves(b)
+    return jnp.concatenate([high, low, high], axis=0)
+
+
+def doubled(b):
+    return jnp.concatenate(halves(b), axis=0)
+
+
+def by_parts(a, bh, bl, dims=NN):
+    n = a.shape[0] // 2
+    both = raw(a, bh, dims)
+    return both[:n] + (both[n:] + raw(a[:n], bl, dims))
 
 
 def mm_exact_b(a, b, dims=NN):
@@ -320,15 +326,15 @@
         else:
             value = across + float(at - CELLS * origin(dx, 2))
         line = jnp.where(code == float(dx * 9 + dy * 3 + dz), value, line)
-    raised = jnp.where(sz != 0.0, KEPT * upper, 0.0)
-    place_j = 9.0 * z_in + 3.0 * atom_j + raised
-    kind_at_j = kind_lane(z_in, atom_j) + raised
+    raised = jnp.where(sz != 0.0, upper, 0.0)
+    place_j = 3.0 * z_in + atom_j + (KEPT // 3) * raised
+    kind_at_j = kind_lane(z_in, atom_j) + KEPT * raised
     inner = jnp.where(code == 0.0, across, -1.0)
 
     tail = jnp.full((1, LANES - centre_total), -8.0, jnp.float32)
     column = jnp.concatenate([inner, col_i, tail], axis=1).astype(jnp.int32)
     place = jnp.concatenate(
-        [jnp.where(code == 0.0, place_j, -8.0), 9.0 * z_i + 3.0 * atom_i, tail], axis=1
+        [jnp.where(code == 0.0, place_j, -8.0), 3.0 * z_i + atom_i, tail], axis=1
     ).astype(jnp.int32)
     kind_at = jnp.concatenate([kind_at_j, kind_lane(z_i, atom_i), tail], axis=1).astype(jnp.int32)
 
@@ -336,17 +342,33 @@
         ids = lax.broadcasted_iota(jnp.int32, (length, index.shape[1]), 0)
         return jnp.where(ids == index, 1.0, 0.0).astype(jnp.bfloat16)
 
+    def third(rows, width):
+        ids = lax.broadcasted_iota(jnp.int32, (rows, width), 0).astype(jnp.float32)
+        group = divided(ids, 3.0)
+        return group.astype(jnp.int32), (ids - 3.0 * group).astype(jnp.int32)
+
     def picked(stack, at, kind_at):
-        ids = lax.broadcasted_iota(jnp.int32, stack.shape, 0)
-        body, body_ids = stack[0:96], ids[0:96]
+        width = stack.shape[1]
+        group, _ = third(96, width)
+        _, turn = third(24, width)
+        kept = jnp.where(group == at, stack[0:96], 0.0)
+        folded = (kept[0:24] + kept[24:48]) + (kept[48:72] + kept[72:96])
         out = [
-            jnp.sum(jnp.where(body_ids == at + c, body, 0.0), axis=0, keepdims=True)
-            for c in range(3)
+            jnp.sum(jnp.where(turn == c, folded, 0.0), axis=0, keepdims=True) for c in range(3)
         ]
-        kind = jnp.sum(
-            jnp.where(ids[88:120] == kind_at, stack[88:120], 0.0), axis=0, keepdims=True
-        )
+        ids = lax.broadcasted_iota(jnp.int32, (32, width), 0) + 88
+        kind = jnp.sum(jnp.where(ids == kind_at, stack[88:120], 0.0), axis=0, keepdims=True)
         return out, kind
+
+    def placed(at, values):
+        width = at.shape[1]
+        group, _ = third(96, width)
+        _, turn = third(24, width)
+        cycle = jnp.where(
+            turn == 0, values[0], jnp.where(turn == 1, values[1], values[2])
+        )
+        out = jnp.where(group == at, jnp.concatenate([cycle] * 4, axis=0), 0.0)
+        return jnp.concatenate([out, jnp.zeros((LANES - 96, width), jnp.float32)], axis=0)
 
     def fetch(block, onehot):
         both = raw(jnp.concatenate(halves(block.T), axis=0), onehot, NN)
@@ -383,7 +405,12 @@
 
     two = w_two[...]
     two = jnp.concatenate([two[4:12], two[0:4], jnp.zeros_like(two[0:4])], axis=0)
-    two_t, lat_t, env_t, out_t = two.T, w_lat[...].T, w_env[...].T, w_out_t[...]
+    out_t = w_out_t[...]
+    width = w_lat.shape[0]
+    two_3, lat_3, env_3 = thrice(two.T), thrice(w_lat[...].T), thrice(w_env[...].T)
+    out_a, out_b = thrice(out_t[:, 0:width]), doubled(out_t[:, width:])
+    back_3 = thrice(out_t.T)
+    gain = jnp.broadcast_to(readout[...], (8, width)).T[:, 0:1]
 
     crossing = plan[-1][1] + plan[-1][2] - 1
     halo_rows = halo.shape[0]
@@ -391,10 +418,6 @@
     def every(ref, send, recv):
         span = pl.ds(0, crossing)
         return remote(ref.at[span], ref.at[span], send, recv, swapped)
-
-    post.wait_recv()
-    arrivals = every(halo, send_a.at[0], recv_a.at[0])
-    arrivals.wait_recv()
 
     ids = lax.broadcasted_iota(jnp.int32, (8, LANES), 0)
 
@@ -408,129 +431,202 @@
         pieces = [block[0:base], tile, block[base + 8 :]]
         return jnp.concatenate([p for p in pieces if p.shape[0]], axis=0)
 
+    arrivals = every(halo, send_a.at[0], recv_a.at[0])
+    wide = 2 * LANES
+    per = wide // slots
+    lines = -(-9 * per // 16) * 16
+    member = (
+        lax.broadcasted_iota(jnp.int32, (per, wide), 1)
+        - slots * lax.broadcasted_iota(jnp.int32, (per, wide), 0)
+    )
+    member = ((member >= 0) & (member < slots)).astype(jnp.float32)
+    unused = jnp.zeros((lines - 9 * per, wide), jnp.float32)
+    spot = lax.broadcasted_iota(jnp.int32, (width, 3 * lines), 1)
+    term = jnp.where(spot >= 2 * lines, 2, jnp.where(spot >= lines, 1, 0))
+    inner_spot = spot - lines * term
+    groups = [
+        (inner_spot >= a * per) & (inner_spot < b * per) for a, b in ((0, 1), (1, 4), (4, 9))
+    ]
+    block_row = lax.broadcasted_iota(jnp.int32, (lines, 3 * width), 0)
+    block_lane = lax.broadcasted_iota(jnp.int32, (lines, 3 * width), 1)
+    blocks = [
+        (block_row >= a * per) & (block_row < b * per) & (block_lane >= k * width)
+        & (block_lane < (k + 1) * width)
+        for k, (a, b) in enumerate(((0, 1), (1, 4), (4, 9)))
+    ]
+    blocks = blocks[0] | blocks[1] | blocks[2]
+    order = (lax.broadcasted_iota(jnp.int32, (NBASIS, wide), 0) + 1).astype(jnp.float32)
+    s3, s5, s15 = math.sqrt(3.0), math.sqrt(5.0), math.sqrt(15.0)
+    norm = math.sqrt(2.0 / CUTOFF)
+
+    def split(a):
+        high = a.astype(jnp.bfloat16).astype(jnp.float32)
+        return jnp.where(term == 2, a - high, high)
+
+    post.wait_recv()
     letter = inbox[...]
+    hot_j = hot(letter[5:6].astype(jnp.int32), halo_rows)
+    there = letter[6:7].astype(jnp.int32)
+    arrivals.wait_recv()
+
     block = with_mine(halo[...], lambda step, at: source(step, 1)[...])
     total_rows = plan[-1][1] + plan[-1][2]
     if total_rows < halo_rows:
         every_id = lax.broadcasted_iota(jnp.int32, (halo_rows, LANES), 0)
         block = jnp.where(every_id < total_rows, block, 0.0)
-    hot_j = hot(letter[5:6].astype(jnp.int32), halo_rows)
-    there = letter[6:7].astype(jnp.int32)
-    shift_j, kind_j = picked(fetch(block, hot_j), there, letter[7:8].astype(jnp.int32))
-    rx, ry, rz = [letter[c : c + 1] + SIDE * shift_j[c] for c in range(3)]
-    live = jnp.where(letter[3:4] > 1.5, 1.0, 0.0)
-    kind_i = letter[3:4] - 2.0 * live
-    kind_j = letter[4:5] + kind_j
-    dist = jnp.sqrt(rx * rx + ry * ry + rz * rz)
-    inv = 1.0 / dist
-    ux, uy, uz = rx * inv, ry * inv, rz * inv
-    ratio = dist * (1.0 / CUTOFF)
-    r2 = ratio * ratio
-    r5 = r2 * r2 * ratio
-    inside = ratio < 1.0
-    bell = jnp.where(inside, 1.0 + r5 * ratio * (-28.0 + ratio * (48.0 - 21.0 * ratio)), 0.0)
-    slope = jnp.where(
-        inside, r5 * (1.0 - ratio) * (1.0 - ratio) * (-168.0 / CUTOFF), 0.0
-    )
-    order = (lax.broadcasted_iota(jnp.int32, (NBASIS, pairs), 0) + 1).astype(jnp.float32)
-    turns = order * (dist * (0.5 / CUTOFF))
-    sines, cosines = wave(turns), wave(turns + 0.25)
-    norm = math.sqrt(2.0 / CUTOFF)
-    basis = norm * sines * (inv * bell)
-    basis_d = norm * (
-        cosines * order * (inv * bell * (math.pi / CUTOFF))
-        + sines * (inv * (slope - bell * inv))
-    )
-    kinds = [1.0 - kind_i, kind_i, 1.0 - kind_j, kind_j]
-    inputs = jnp.concatenate([basis] + kinds + [jnp.zeros((4, pairs), jnp.float32)], axis=0)
-
-    hidden, hidden_d = silu_pair(mm(two_t, inputs))
-    latent, latent_d = silu_pair(mm(lat_t, hidden))
-    latent_h = halves(latent)
-    plain = mm(env_t, latent_h)
-    scale = bell * live
-    weight = plain * scale
-    s3, s5, s15 = math.sqrt(3.0), math.sqrt(5.0), math.sqrt(15.0)
-    harm = [
-        jnp.ones_like(ux),
-        s3 * ux,
-        s3 * uy,
-        s3 * uz,
-        s15 * ux * uy,
-        s15 * uy * uz,
-        0.5 * s5 * (3.0 * uz * uz - 1.0),
-        s15 * ux * uz,
-        0.5 * s15 * (ux * ux - uy * uy),
-    ]
-    spread_y = halves(jnp.concatenate([h * mine for h in harm], axis=0))
-    weight_h = halves(weight)
-    bounds = [(0, 1), (1, 4), (4, 9)]
-    cuts = [slice(a * centre_total, b * centre_total) for a, b in bounds]
-
-    def cut(pair, s):
-        return pair[0][s], pair[1][s]
-
-    environ = ENV * mm(spread_y, weight_h, NT)
-    mixed = [mm(environ[s].T, cut(spread_y, s)) for s in cuts]
-    width = latent.shape[0]
-    joined = jnp.concatenate([latent] + [weight * a for a in mixed], axis=0)
-    updated, updated_d = silu_pair(mm(out_t, joined))
-    gain = jnp.broadcast_to(readout[...], (8, width)).T[:, 0:1]
-    score = jnp.sum(gain * updated, axis=0, keepdims=True)
-    pair_energy = score * scale
-
-    d_out = (gain * scale) * updated_d
-    back = mm(out_t.T, d_out)
-    d_mixed = [back[width * (k + 1) : width * (k + 2)] for k in range(3)]
-    d_weight = d_mixed[0] * mixed[0] + d_mixed[1] * mixed[1] + d_mixed[2] * mixed[2]
-    passing = [halves(q * weight) for q in d_mixed]
-    d_environ = ENV * jnp.concatenate(
-        [mm(cut(spread_y, s), p, NT) for s, p in zip(cuts, passing)], axis=0
-    )
-    d_weight = d_weight + mm(d_environ.T, spread_y)
-    d_spread = jnp.concatenate(
-        [mm(environ[s], p) for s, p in zip(cuts, passing)], axis=0
-    ) + mm(d_environ, weight_h)
-    d_harm = [
-        jnp.sum(
-            d_spread[m * centre_total : (m + 1) * centre_total] * mine, axis=0, keepdims=True
-        )
-        for m in range(9)
-    ]
-    d_scale = score + jnp.sum(d_weight * plain, axis=0, keepdims=True)
-    d_latent = back[0:width] + mm(w_env[...], d_weight * scale)
-    d_hidden = mm(w_lat[...], d_latent * latent_d)
-    d_inputs = mm(two, d_hidden * hidden_d)
-    d_dist = (
-        jnp.sum(d_inputs[0:NBASIS] * basis_d, axis=0, keepdims=True) + d_scale * live * slope
-    )
-    dux = s3 * d_harm[1] + s15 * (uy * d_harm[4] + uz * d_harm[7] + ux * d_harm[8])
-    duy = s3 * d_harm[2] + s15 * (ux * d_harm[4] + uz * d_harm[5] - uy * d_harm[8])
-    duz = s3 * d_harm[3] + s15 * (uy * d_harm[5] + ux * d_harm[7]) + 3.0 * s5 * uz * d_harm[6]
-    radial = d_dist - (ux * dux + uy * duy + uz * duz) * inv
-    grad = [d * inv + u * radial for d, u in ((dux, ux), (duy, uy), (duz, uz))]
-
-
-    back_mail[0:3, 0:pairs] = jnp.concatenate(grad, axis=0)
+    block = doubled(block.T)
+
+    def network(at):
+        note = letter[:, at : at + wide]
+        both = raw(block, hot_j[:, at : at + wide], NN)
+        yield
+        shift_j, kind_j = picked(
+            both[:LANES] + both[LANES:], there[:, at : at + wide], note[7:8].astype(jnp.int32)
+        )
+        yield
+        rx, ry, rz = [note[c : c + 1] + SIDE * shift_j[c] for c in range(3)]
+        live = jnp.where(note[3:4] > 1.5, 1.0, 0.0)
+        kind_i = note[3:4] - 2.0 * live
+        kind_j = note[4:5] + kind_j
+        dist = jnp.sqrt(rx * rx + ry * ry + rz * rz)
+        inv = 1.0 / dist
+        ux, uy, uz = rx * inv, ry * inv, rz * inv
+        ratio = dist * (1.0 / CUTOFF)
+        r2 = ratio * ratio
+        r5 = r2 * r2 * ratio
+        inside = ratio < 1.0
+        bell = jnp.where(
+            inside, 1.0 + r5 * ratio * (-28.0 + ratio * (48.0 - 21.0 * ratio)), 0.0
+        )
+        slope = jnp.where(
+            inside, r5 * (1.0 - ratio) * (1.0 - ratio) * (-168.0 / CUTOFF), 0.0
+        )
+        turns = order * (dist * (0.5 / CUTOFF))
+        sines, cosines = wave(turns), wave(turns + 0.25)
+        basis = norm * sines * (inv * bell)
+        basis_d = norm * (
+            cosines * order * (inv * bell * (math.pi / CUTOFF))
+            + sines * (inv * (slope - bell * inv))
+        )
+        kinds = [1.0 - kind_i, kind_i, 1.0 - kind_j, kind_j]
+        inputs = jnp.concatenate(
+            [basis] + kinds + [jnp.zeros((4, wide), jnp.float32)], axis=0
+        )
+        inputs_t = jnp.concatenate([basis_d, jnp.zeros((8, wide), jnp.float32)], axis=0)
+
+        hidden = raw(two_3, stacked(inputs), NN)
+        hidden_t = raw(two_3, stacked(inputs_t), NN)
+        yield
+        hidden, hidden_d = silu_pair(hidden)
+        latent = raw(lat_3, stacked(hidden), NN)
+        latent_t = raw(lat_3, stacked(hidden_t * hidden_d), NN)
+        yield
+        latent, latent_d = silu_pair(latent)
+        latent_t = latent_t * latent_d
+        lat_h, lat_l = halves(latent)
+        scale = bell * live
+        scale_t = slope * live
+        harm = [
+            jnp.ones_like(ux),
+            s3 * ux,
+            s3 * uy,
+            s3 * uz,
+            s15 * ux * uy,
+            s15 * uy * uz,
+            0.5 * s5 * (3.0 * uz * uz - 1.0),
+            s15 * ux * uz,
+            0.5 * s15 * (ux * ux - uy * uy),
+        ]
+        rows = jnp.concatenate([h * member for h in harm] + [unused], axis=0)
+        rows_h, rows_l = halves(rows)
+        rows_3 = jnp.concatenate([rows_h, rows_l, rows_h], axis=0)
+        scaled_h, scaled_l = [
+            jnp.concatenate([v] * 3, axis=0) for v in halves(rows * scale)
+        ]
+        gathered = by_parts(jnp.concatenate([lat_h, lat_l], axis=0), scaled_h, scaled_l, NT)
+        yield
+        environ = ENV * raw(env_3, stacked(gathered), NN)
+        lat_s = jnp.concatenate([lat_h, lat_l, lat_h], axis=0)
+        plain = raw(env_3, lat_s, NN)
+        yield
+        environ_s = split(environ)
+        chosen = jnp.concatenate(
+            [jnp.where(g, environ_s, 0.0) for g in groups], axis=0
+        ).astype(jnp.bfloat16)
+        mixed = raw(chosen, rows_3, NN)
+        partly = raw(out_a, lat_s, NN)
+        plain_t = raw(env_3, stacked(latent_t), NN)
+        weight = plain * scale
+        yield
+        mixed = [mixed[width * k : width * (k + 1)] for k in range(3)]
+        joined_h, joined_l = halves(jnp.concatenate([weight * a for a in mixed], axis=0))
+        updated = by_parts(out_b, joined_h, joined_l) + partly
+        yield
+        weight_t = plain_t * scale + plain * scale_t
+        near = jnp.concatenate([jnp.where(g, environ, 0.0)[:, 0:LANES] for g in groups], axis=0)
+        near = doubled(near.T[0:lines])
+        (weight_h, weight_l), (slant_h, slant_l) = halves(weight), halves(weight_t)
+        updated, updated_d = silu_pair(updated)
+        d_out = (gain * scale) * updated_d
+        back = raw(back_3, stacked(d_out), NN)
+        score = jnp.sum(gain * updated, axis=0, keepdims=True)
+        pair_energy = score * scale
+        yield
+        d_mixed = [back[width * (k + 1) : width * (k + 2)] for k in range(3)]
+        pass_h, pass_l = halves(jnp.concatenate([q * weight for q in d_mixed], axis=0))
+        d_env = by_parts(jnp.concatenate([rows_h, rows_l], axis=0), pass_h, pass_l, NT)
+        d_rows = by_parts(near, pass_h, pass_l)
+        yield
+        along = d_mixed[0] * mixed[0] + d_mixed[1] * mixed[1] + d_mixed[2] * mixed[2]
+        d_dist = (
+            jnp.sum(along * weight_t + back[0:width] * latent_t, axis=0, keepdims=True)
+            + score * scale_t
+        )
+        d_env = doubled(jnp.where(blocks, ENV * d_env, 0.0))
+        d_rows = d_rows + by_parts(
+            d_env,
+            jnp.concatenate([weight_h] * 3, axis=0),
+            jnp.concatenate([weight_l] * 3, axis=0),
+        )
+        slanted = by_parts(
+            d_env,
+            jnp.concatenate([slant_h] * 3, axis=0),
+            jnp.concatenate([slant_l] * 3, axis=0),
+        )
+        yield
+        d_harm = [
+            jnp.sum(d_rows[m * per : (m + 1) * per] * member, axis=0, keepdims=True)
+            for m in range(9)
+        ]
+        d_dist = d_dist + jnp.sum(rows * slanted, axis=0, keepdims=True)
+        dux = s3 * d_harm[1] + s15 * (uy * d_harm[4] + uz * d_harm[7] + ux * d_harm[8])
+        duy = s3 * d_harm[2] + s15 * (ux * d_harm[4] + uz * d_harm[5] - uy * d_harm[8])
+        duz = (
+            s3 * d_harm[3]
+            + s15 * (uy * d_harm[5] + ux * d_harm[7])
+            + 3.0 * s5 * uz * d_harm[6]
+        )
+        radial = d_dist - (ux * dux + uy * duy + uz * duz) * inv
+        yield [d * inv + u * radial for d, u in ((dux, ux), (duy, uy), (duz, uz))] + [
+            pair_energy
+        ]
+
+    runs = [network(at) for at in range(0, pairs, wide)]
+    found = [None] * len(runs)
+    while found[0] is None:
+        found = [next(run) for run in runs]
+    *grad, pair_energy = [jnp.concatenate(v, axis=1) for v in zip(*found)]
     sums = mm_exact_b(
         jnp.concatenate(grad + [pair_energy, jnp.zeros((4, pairs), jnp.float32)], axis=0),
         mine16,
         NT,
     )
+    partial = mm_exact_a(hot_j, placed(there, [-g for g in grad]))
+    back_mail[0:3, 0:pairs] = jnp.concatenate(grad, axis=0)
     back_mail[:, pairs : pairs + centre_total] = sums[0:4]
     reply = remote(back_mail, back_inbox, send_b.at[1], recv_b.at[1], swapped)
     reply.start()
-
-    def placed(at, values):
-        ids = lax.broadcasted_iota(jnp.int32, (96, at.shape[1]), 0)
-        out = jnp.zeros(ids.shape, jnp.float32)
-        for c in range(3):
-            out = jnp.where(ids == at + c, values[c], out)
-        return jnp.concatenate(
-            [out, jnp.zeros((LANES - 96, at.shape[1]), jnp.float32)], axis=0
-        )
-
-    part[...] = mm_exact_a(hot_j, placed(there, [-g for g in grad]))
+    part[...] = partial
     for step, at, rows in reversed(plan):
         span = pl.ds(at, rows)
         copy = remote(part.at[span], got.at[span], send_b.at[0], recv_b.at[0], holder(step))

time: 18.8 us -> 17.4 us (0.926)
  Pallas kernels: 17.4 us -> 15.9 us
    pallas_call x1, Pallas kernels: 16.7 us -> 15.3 us  [local(): pl.pallas_call(body, out_shape=pltpu.VMEM((CELLS * CELLS + 8, LANES), jnp...]
where the time goes in v3:
time: 17.4 us; the launch traced here: 17.2 us
  Pallas kernels  15.9 us (91%)
  between operations  1.29 us (7%)
    pallas_call x1, Pallas kernels, local(): pl.pallas_call(body, out_shape=pltpu.VMEM((CELLS * CELLS + 8, LANES), jnp...  15.3 us
    pallas_call x1, Pallas kernels, local(): pl.pallas_call(unpack_body, out_shape=(jax.ShapeDtypeStruct(centres.shape...  0.7 us

profile of v3, /device:TPU:0, one launch (start us, length us, event | category | flops | bytes accessed | tf_op | source)
XLA Modules:
  0.0 17.2 jit_solution(13641709330096776812)
XLA Ops:
  1.3 15.3 %shard_map.122.result = f32[72,128]{1,0:T(8,128)S(1)} custom-call(f32[1,1,4608]{2,1,0:T(1,128)} %refs_0_.1, s32[1,1,1536]{2,1,0:T(1,128)} %refs_1_.1, s32[1,1,16]{2,1,0:T(1,128)} %refs_2_.1, s32[1,1,512]{2,1,0:T(1,128)} %refs_3_.1, s32[1,1,16]{2,1,0:T(1,128)} %refs_4_.1, s32[1,1,1]{2,1,0:T(1,128)S(6)} %copy.13.refs_5_, f32[12,64]{1,0:T(8,128)} %refs_6_.1, ...), custom_call_target="tpu_custom_call" | custom-call | tf_op jit(solution)/shard_map/pallas_call | solution.py:712
  16.5 0.7 %shard_map.123 = (f32[1,1,16]{2,1,0:T(1,128)}, f32[1,1,4608]{2,1,0:T(1,128)}) custom-call(f32[72,128]{1,0:T(8,128)S(1)} %shard_map.122.result), custom_call_target="tpu_custom_call" | custom-call | tf_op jit(solution)/shard_map/pallas_call | solution.py:724

commit v4 on v3

--- a/solution.py
+++ b/solution.py
@@ -88,6 +88,14 @@
     return 0 if step >= 0 else CELLS - tiles
 
 
+def by_reach(plan):
+    def rank(entry):
+        (dx, dy, dz), _, rows = entry
+        return dy == 0, dy < 0, rows > CELLS, dz, rows
+
+    return sorted(plan, key=rank)
+
+
 def own_corner(step):
     return step[2] == 0 and step[0] != 0 and step[1] != 0
 
@@ -108,14 +116,14 @@
 
 
 def silu_pair(x):
-    s = 1.0 / (1.0 + jnp.exp(-x))
+    s = 0.5 + 0.5 * jnp.tanh(0.5 * x)
     return x * s, s * (1.0 + x * (1.0 - s))
 
 
 def kernel_body(sizes, plan, disp_hbm, spec_hbm, cen_hbm, nbr_hbm, cnt_hbm, alive_hbm, two_hbm,
                 lat_hbm, env_hbm, out_hbm, readout_hbm, result,
                 disp, spec, cen, nbr, cnt, alive, w_two, w_lat, w_env, w_out_t, readout,
-                table, pack, ztable, zpack, mail, inbox, back_mail, back_inbox, halo, part, got,
+                table, pack, ztable, zpack, note, inbox, mail, mail_in, back_mail, back_inbox, halo, part, got,
                 send_a, recv_a, send_b, recv_b, load):
     loads = [
         pltpu.make_async_copy(src, dst, load.at[at])
@@ -173,11 +181,11 @@
         else:
             action()
 
-    for step, at, rows in reversed(plan):
+    for step, at, rows in by_reach(plan):
         unless_mine(step, lambda step=step: greet(holder(step)))
     greet(swapped)
 
-    for copy in loads[:2]:
+    for copy in loads[:6]:
         copy.wait()
     dwide, swide = 16 * ZROWS, 16 * KINDS
     dline = jnp.concatenate([disp[:, dwide * q : dwide * (q + 1)] for q in range(4)], axis=0)
@@ -239,15 +247,6 @@
             device_id_type=pl.DeviceIdType.MESH,
         )
 
-    pl.semaphore_wait(barrier, len(plan))
-    for step, at, rows in reversed(plan):
-        copy = remote(
-            source(step, rows), halo.at[pl.ds(at, rows)], send_a.at[0], recv_a.at[0], worker(step)
-        )
-        unless_mine(step, copy.start)
-
-    for copy in loads[2:]:
-        copy.wait()
 
     pairs = nbr.shape[1]
     centre_total = cen.shape[1]
@@ -282,7 +281,9 @@
     count = jnp.where(alive_lane < alive[...], cnt[...], 0).astype(jnp.float32)
     spread = raw(
         jnp.concatenate(
-            spot_i + [count, jnp.zeros((4, centre_total), jnp.float32)], axis=0
+            spot_i + [count, col_i, 3.0 * z_i + atom_i, kind_lane(z_i, atom_i)]
+            + [jnp.zeros((1, centre_total), jnp.float32)],
+            axis=0,
         ).astype(jnp.bfloat16),
         mine16,
         NN,
@@ -331,12 +332,11 @@
     kind_at_j = kind_lane(z_in, atom_j) + KEPT * raised
     inner = jnp.where(code == 0.0, across, -1.0)
 
-    tail = jnp.full((1, LANES - centre_total), -8.0, jnp.float32)
-    column = jnp.concatenate([inner, col_i, tail], axis=1).astype(jnp.int32)
     place = jnp.concatenate(
-        [jnp.where(code == 0.0, place_j, -8.0), 3.0 * z_i + atom_i, tail], axis=1
+        [jnp.where(code == 0.0, place_j, -8.0), spread[5:6]], axis=1
     ).astype(jnp.int32)
-    kind_at = jnp.concatenate([kind_at_j, kind_lane(z_i, atom_i), tail], axis=1).astype(jnp.int32)
+    kind_at = jnp.concatenate([kind_at_j, spread[6:7]], axis=1).astype(jnp.int32)
+    column = jnp.concatenate([inner, spread[4:5]], axis=1).astype(jnp.int32)
 
     def hot(index, length):
         ids = lax.broadcasted_iota(jnp.int32, (length, index.shape[1]), 0)
@@ -371,38 +371,40 @@
         return jnp.concatenate([out, jnp.zeros((LANES - 96, width), jnp.float32)], axis=0)
 
     def fetch(block, onehot):
-        both = raw(jnp.concatenate(halves(block.T), axis=0), onehot, NN)
-        return both[:LANES] + both[LANES:]
+        return raw(
+            jnp.concatenate(halves(block.T), axis=1),
+            jnp.concatenate([onehot, onehot], axis=0),
+            NN,
+        )
 
     hot_own = hot(column, own)
+    note[...] = jnp.concatenate([line, place_j, kind_at_j, live], axis=0)
+    spot_j = [a + b for a, b in zip((x_j, y_j, z_j), site(atom_j))]
+    apart = [spot_j[c] - spread[c : c + 1] for c in range(3)]
+
+    pl.semaphore_wait(barrier, len(plan))
+    post = None
+    for step, at, rows in by_reach(plan):
+        if step[1] == 0 and post is None:
+            post = remote(note, inbox, send_a.at[1], recv_a.at[1], worker((0, 0, 0)))
+            post.start()
+        copy = remote(
+            source(step, rows), halo.at[pl.ds(at, rows)], send_a.at[0], recv_a.at[0], worker(step)
+        )
+        unless_mine(step, copy.start)
+
+
     shift, kind = picked(fetch(table[...], hot_own), place, kind_at)
-    from_centre = mm_exact_b(
-        jnp.concatenate(
-            [v[:, pairs : pairs + centre_total] for v in shift + [kind]]
-            + [jnp.zeros((4, centre_total), jnp.float32)],
-            axis=0,
-        ),
-        mine16,
-    )
-    spot_j = [a + b for a, b in zip((x_j, y_j, z_j), site(atom_j))]
     mail[...] = jnp.concatenate(
-        [
-            ((spot_j[c] - spread[c : c + 1]) + (shift[c][:, 0:pairs] - from_centre[c : c + 1]))
-            * SIDE
-            for c in range(3)
-        ]
-        + [
-            from_centre[3:4] + 2.0 * live,
-            jnp.where(code == 0.0, kind[:, 0:pairs], 0.0),
-            line,
-            place_j,
-            kind_at_j,
-        ],
+        [(apart[c] + (shift[c][:, 0:pairs] - shift[c][:, pairs:])) * SIDE for c in range(3)]
+        + [kind[:, pairs:] + 2.0 * jnp.where(code == 0.0, kind[:, 0:pairs], 0.0)],
         axis=0,
     )
-    post = remote(mail, inbox, send_a.at[1], recv_a.at[1], worker((0, 0, 0)))
-    post.start()
-
+    parcel = remote(mail, mail_in, send_a.at[2], recv_a.at[2], worker((0, 0, 0)))
+    parcel.start()
+
+    for copy in loads[6:]:
+        copy.wait()
     two = w_two[...]
     two = jnp.concatenate([two[4:12], two[0:4], jnp.zeros_like(two[0:4])], axis=0)
     out_t = w_out_t[...]
@@ -422,14 +424,16 @@
     ids = lax.broadcasted_iota(jnp.int32, (8, LANES), 0)
 
     def with_mine(block, row_of):
-        pieces = block
         corner = [(step, at) for step, at, rows in plan if own_corner(step)]
         base = corner[0][1] // 8 * 8
         tile = block[base : base + 8]
         for step, at in corner:
             tile = jnp.where((ids == at - base) & mine_too(step), row_of(step, at), tile)
-        pieces = [block[0:base], tile, block[base + 8 :]]
-        return jnp.concatenate([p for p in pieces if p.shape[0]], axis=0)
+        pieces = [block[0:base]] if base else []
+        pieces.append(tile)
+        if base + 8 < block.shape[0]:
+            pieces.append(block[base + 8 :])
+        return jnp.concatenate(pieces, axis=0)
 
     arrivals = every(halo, send_a.at[0], recv_a.at[0])
     wide = 2 * LANES
@@ -465,8 +469,10 @@
 
     post.wait_recv()
     letter = inbox[...]
-    hot_j = hot(letter[5:6].astype(jnp.int32), halo_rows)
-    there = letter[6:7].astype(jnp.int32)
+    hot_j = hot(letter[0:1].astype(jnp.int32), halo_rows)
+    twice_j = jnp.concatenate([hot_j, hot_j], axis=0)
+    there = letter[1:2].astype(jnp.int32)
+    kind_there = letter[2:3].astype(jnp.int32)
     arrivals.wait_recv()
 
     block = with_mine(halo[...], lambda step, at: source(step, 1)[...])
@@ -474,22 +480,25 @@
     if total_rows < halo_rows:
         every_id = lax.broadcasted_iota(jnp.int32, (halo_rows, LANES), 0)
         block = jnp.where(every_id < total_rows, block, 0.0)
-    block = doubled(block.T)
+
+    block = jnp.concatenate([v.T for v in halves(block)], axis=1)
+
+    stacks = [raw(block, twice_j[:, at : at + wide], NN) for at in range(0, pairs, wide)]
+    parcel.wait_recv()
+    sheet = mail_in[...]
 
     def network(at):
-        note = letter[:, at : at + wide]
-        both = raw(block, hot_j[:, at : at + wide], NN)
-        yield
-        shift_j, kind_j = picked(
-            both[:LANES] + both[LANES:], there[:, at : at + wide], note[7:8].astype(jnp.int32)
-        )
-        yield
-        rx, ry, rz = [note[c : c + 1] + SIDE * shift_j[c] for c in range(3)]
-        live = jnp.where(note[3:4] > 1.5, 1.0, 0.0)
-        kind_i = note[3:4] - 2.0 * live
-        kind_j = note[4:5] + kind_j
-        dist = jnp.sqrt(rx * rx + ry * ry + rz * rz)
-        inv = 1.0 / dist
+        span = slice(at, at + wide)
+        shift_j, kind_j = picked(stacks[at // wide], there[:, span], kind_there[:, span])
+        yield
+        rx, ry, rz = [sheet[c : c + 1, span] + SIDE * shift_j[c] for c in range(3)]
+        live = letter[3:4, span]
+        own_j = jnp.where(sheet[3:4, span] > 1.5, 1.0, 0.0)
+        kind_i = sheet[3:4, span] - 2.0 * own_j
+        kind_j = own_j + kind_j
+        square = rx * rx + ry * ry + rz * rz
+        inv = lax.rsqrt(square)
+        dist = square * inv
         ux, uy, uz = rx * inv, ry * inv, rz * inv
         ratio = dist * (1.0 / CUTOFF)
         r2 = ratio * ratio
@@ -565,7 +574,7 @@
         weight_t = plain_t * scale + plain * scale_t
         near = jnp.concatenate([jnp.where(g, environ, 0.0)[:, 0:LANES] for g in groups], axis=0)
         near = doubled(near.T[0:lines])
-        (weight_h, weight_l), (slant_h, slant_l) = halves(weight), halves(weight_t)
+        weight_s, slant_s = stacked(weight), stacked(weight_t)
         updated, updated_d = silu_pair(updated)
         d_out = (gain * scale) * updated_d
         back = raw(back_3, stacked(d_out), NN)
@@ -582,30 +591,26 @@
             jnp.sum(along * weight_t + back[0:width] * latent_t, axis=0, keepdims=True)
             + score * scale_t
         )
-        d_env = doubled(jnp.where(blocks, ENV * d_env, 0.0))
-        d_rows = d_rows + by_parts(
-            d_env,
-            jnp.concatenate([weight_h] * 3, axis=0),
-            jnp.concatenate([weight_l] * 3, axis=0),
-        )
-        slanted = by_parts(
-            d_env,
-            jnp.concatenate([slant_h] * 3, axis=0),
-            jnp.concatenate([slant_l] * 3, axis=0),
-        )
-        yield
-        d_harm = [
-            jnp.sum(d_rows[m * per : (m + 1) * per] * member, axis=0, keepdims=True)
-            for m in range(9)
+        d_env = jnp.where(blocks, ENV * d_env, 0.0)
+        d_env = jnp.concatenate([d_env, jnp.zeros((lines, width), jnp.float32)], axis=1)
+        d_env = d_env[:, 0:LANES] + d_env[:, LANES:]
+        d_env_h, d_env_l = halves(d_env + pltpu.roll(d_env, width, 1))
+        d_env = jnp.concatenate([d_env_h, d_env_l[:, 0:width]], axis=1)
+        d_rows = d_rows + raw(d_env, weight_s, NN)
+        slanted = raw(d_env, slant_s, NN)
+        yield
+        turned = [d_rows[m * per : (m + 1) * per] for m in range(9)]
+        dux = s3 * turned[1] + s15 * (uy * turned[4] + uz * turned[7] + ux * turned[8])
+        duy = s3 * turned[2] + s15 * (ux * turned[4] + uz * turned[5] - uy * turned[8])
+        duz = (
+            s3 * turned[3]
+            + s15 * (uy * turned[5] + ux * turned[7])
+            + 3.0 * s5 * uz * turned[6]
+        )
+        dux, duy, duz = [
+            jnp.sum(d * member, axis=0, keepdims=True) for d in (dux, duy, duz)
         ]
         d_dist = d_dist + jnp.sum(rows * slanted, axis=0, keepdims=True)
-        dux = s3 * d_harm[1] + s15 * (uy * d_harm[4] + uz * d_harm[7] + ux * d_harm[8])
-        duy = s3 * d_harm[2] + s15 * (ux * d_harm[4] + uz * d_harm[5] - uy * d_harm[8])
-        duz = (
-            s3 * d_harm[3]
-            + s15 * (uy * d_harm[5] + ux * d_harm[7])
-            + 3.0 * s5 * uz * d_harm[6]
-        )
         radial = d_dist - (ux * dux + uy * duy + uz * duz) * inv
         yield [d * inv + u * radial for d, u in ((dux, ux), (duy, uy), (duz, uz))] + [
             pair_energy
@@ -616,64 +621,81 @@
     while found[0] is None:
         found = [next(run) for run in runs]
     *grad, pair_energy = [jnp.concatenate(v, axis=1) for v in zip(*found)]
-    sums = mm_exact_b(
-        jnp.concatenate(grad + [pair_energy, jnp.zeros((4, pairs), jnp.float32)], axis=0),
-        mine16,
-        NT,
-    )
-    partial = mm_exact_a(hot_j, placed(there, [-g for g in grad]))
-    back_mail[0:3, 0:pairs] = jnp.concatenate(grad, axis=0)
-    back_mail[:, pairs : pairs + centre_total] = sums[0:4]
+    back_mail[...] = jnp.concatenate(grad + [pair_energy], axis=0)
     reply = remote(back_mail, back_inbox, send_b.at[1], recv_b.at[1], swapped)
     reply.start()
+    partial = mm_exact_a(hot_j, placed(there, [-g for g in grad]))
     part[...] = partial
-    for step, at, rows in reversed(plan):
+    for step, at, rows in by_reach(plan):
         span = pl.ds(at, rows)
         copy = remote(part.at[span], got.at[span], send_b.at[0], recv_b.at[0], holder(step))
         unless_mine(step, copy.start)
 
     reply.wait_recv()
     answer = back_inbox[...]
-    signs = jnp.where(
-        lax.broadcasted_iota(jnp.int32, (1, pairs + LANES), 1) < pairs, -1.0, 1.0
+    moves = [answer[c : c + 1] for c in range(3)]
+    settled = mm_exact_a(
+        hot_own,
+        jnp.concatenate(
+            [placed(place[:, 0:pairs], [-m for m in moves]), placed(place[:, pairs:], moves)],
+            axis=1,
+        ),
     )
-    total[...] = mm_exact_a(
-        hot_own, placed(place, [signs * answer[c : c + 1] for c in range(3)])
-    )
-    result[pl.ds(own, 8), 0:centre_total] = jnp.broadcast_to(
-        answer[3:4, pairs : pairs + centre_total], (8, centre_total)
-    )
+    energies = mm_exact_b(jnp.broadcast_to(answer[3:4], (8, pairs)), mine16, NT)
+    result[pl.ds(own, 8), 0:centre_total] = energies
+    below = lax.broadcasted_iota(jnp.int32, (CELLS, LANES), 0)
+    upper_lanes = high((CELLS, LANES))
     returns = every(got, send_b.at[0], recv_b.at[0])
     returns.wait_recv()
 
-    def add(spot, value):
-        total[spot, :] = total[spot, :] + value
+    slabs = [settled[CELLS * x : CELLS * (x + 1)] for x in range(CELLS)]
+    columns = {y: [[] for x in range(CELLS)] for y in (0, 1, CELLS - 2, CELLS - 1)}
+
+    def low_part(value):
+        return jnp.where(upper_lanes[0 : value.shape[0]], 0.0, value)
+
+    def high_part(value):
+        kept = jnp.where(upper_lanes[0 : value.shape[0]], value, 0.0)
+        return pltpu.roll(kept, LANES - KEPT, 1)
 
     for (dx, dy, dz), at, rows in plan:
-        value = got[pl.ds(at, rows), :]
         x, y = (CELLS - 1) * (dx < 0), (CELLS - 1) * (dy < 0)
         if own_corner((dx, dy, dz)):
-            value = jnp.where(mine_too((dx, dy, dz)), part[pl.ds(at, 1), :], value)
-            add(pl.ds(CELLS * x + y, 1), value)
+            value = jnp.where(
+                mine_too((dx, dy, dz)), part[pl.ds(at, 1), :], got[pl.ds(at, 1), :]
+            )
+            columns[y][x].append(value)
+        elif dx and dy:
+            value = got[pl.ds(at, 1), :]
+            columns[y][x].append(high_part(value) if dx < 0 else low_part(value))
+        elif dz and dy:
+            value = got[pl.ds(at, rows), :]
+            for part_of, base in ((low_part(value), 0), (high_part(value), rows)):
+                for r in range(rows):
+                    columns[y][base + r].append(part_of[r : r + 1])
+        elif dz and dx:
+            value = got[pl.ds(at, rows), :]
+            slabs[x] = slabs[x] + (high_part(value) if dx < 0 else low_part(value))
         elif dz:
-            top = high(value.shape)
-            low = jnp.where(top, 0.0, value)
-            lifted = pltpu.roll(jnp.where(top, value, 0.0), LANES - KEPT, 1)
-            if dx:
-                spot = pl.ds(CELLS * x + y, rows)
-                add(spot, lifted if dx < 0 else low)
-            elif dy:
-                add(pl.ds(y, rows, stride=CELLS), low)
-                add(pl.ds(HALF + y, rows, stride=CELLS), lifted)
-            else:
-                add(pl.ds(0, HALF), low)
-                add(pl.ds(HALF, HALF), lifted)
+            for r in range(CELLS // 2):
+                value = got[pl.ds(at + CELLS * r, CELLS), :]
+                slabs[r] = slabs[r] + low_part(value)
+                slabs[CELLS // 2 + r] = slabs[CELLS // 2 + r] + high_part(value)
         elif dy:
             for t in range(2):
-                add(pl.ds(origin(dy, 2) + t, 8, stride=8), value[8 * t : 8 * t + 8])
+                for r in range(CELLS):
+                    columns[origin(dy, 2) + t][r].append(got[pl.ds(at + 8 * t + r, 1), :])
         else:
-            add(pl.ds(CELLS * origin(dx, 2), rows), value)
-    for copy in (post, arrivals, reply, returns):
+            for t in range(2):
+                x = origin(dx, 2) + t
+                slabs[x] = slabs[x] + got[pl.ds(at + CELLS * t, CELLS), :]
+    for x in range(CELLS):
+        side = jnp.zeros((CELLS, LANES), jnp.float32)
+        for y, lists in columns.items():
+            value = sum(lists[x][1:], lists[x][0])
+            side = jnp.where(below == y, value, side)
+        total[pl.ds(CELLS * x, CELLS), :] = slabs[x] + side
+    for copy in (post, parcel, arrivals, reply, returns):
         copy.wait_send()
 
 
@@ -702,11 +724,14 @@
         ]
 
         def body(*refs):
-            kernel_body(sizes, plan, *refs)
+            pl.run_scoped(
+                lambda load: kernel_body(sizes, plan, *refs, load),
+                pltpu.SemaphoreType.DMA((len(args),)),
+            )
 
         sizes_vmem = [
             (CELLS * CELLS, LANES), (4 * CELLS, LANES), (HALF, LANES), (CELLS, LANES),
-            (8, pairs), (8, pairs), (4, pairs + LANES), (4, pairs + LANES),
+            (4, pairs), (4, pairs), (4, pairs), (4, pairs), (4, pairs), (4, pairs),
             (rows, LANES), (rows, LANES), (rows, LANES),
         ]
         result = pl.pallas_call(
@@ -716,8 +741,8 @@
             out_specs=vmem,
             scratch_shapes=[pltpu.VMEM(x.shape, x.dtype) for x in args]
             + [pltpu.VMEM(shape, jnp.float32) for shape in sizes_vmem]
-            + [pltpu.SemaphoreType.DMA((2,))] * 4
-            + [pltpu.SemaphoreType.DMA((len(args),))],
+            + [pltpu.SemaphoreType.DMA((3,))] * 2
+            + [pltpu.SemaphoreType.DMA((2,))] * 2,
             compiler_params=pltpu.CompilerParams(collective_id=0, has_side_effects=True),
         )(*args)
         result = pltpu.with_memory_space_constraint(result, pltpu.VMEM)

time: 17.4 us -> 17.1 us (0.983)
  Pallas kernels: 15.9 us -> 15.7 us
    pallas_call x1, Pallas kernels: 15.3 us -> 15 us  [local(): pl.pallas_call(body, out_shape=pltpu.VMEM((CELLS * CELLS + 8, LANES), jnp...]
where the time goes in v4:
time: 17.1 us; the launch traced here: 16.9 us
  Pallas kernels  15.7 us (92%)
  between operations  1.29 us (8%)
    pallas_call x1, Pallas kernels, local(): pl.pallas_call(body, out_shape=pltpu.VMEM((CELLS * CELLS + 8, LANES), jnp...  15 us
    pallas_call x1, Pallas kernels, local(): pl.pallas_call(unpack_body, out_shape=(jax.ShapeDtypeStruct(centres.shape...  0.7 us

profile of v4, /device:TPU:0, one launch (start us, length us, event | category | flops | bytes accessed | tf_op | source)
XLA Modules:
  0.0 16.9 jit_solution(6975350013579418665)
XLA Ops:
  1.3 15.0 %shard_map.122.result = f32[72,128]{1,0:T(8,128)S(1)} custom-call(f32[1,1,4608]{2,1,0:T(1,128)} %refs_0_.1, s32[1,1,1536]{2,1,0:T(1,128)} %refs_1_.1, s32[1,1,16]{2,1,0:T(1,128)} %refs_2_.1, s32[1,1,512]{2,1,0:T(1,128)} %refs_3_.1, s32[1,1,16]{2,1,0:T(1,128)} %refs_4_.1, s32[1,1,1]{2,1,0:T(1,128)S(6)} %copy.13.refs_5_, f32[12,64]{1,0:T(8,128)} %refs_6_.1, ...), custom_call_target="tpu_custom_call" | custom-call | tf_op jit(solution)/shard_map/pallas_call | solution.py:737
  16.2 0.7 %shard_map.123 = (f32[1,1,16]{2,1,0:T(1,128)}, f32[1,1,4608]{2,1,0:T(1,128)}) custom-call(f32[72,128]{1,0:T(8,128)S(1)} %shard_map.122.result), custom_call_target="tpu_custom_call" | custom-call | tf_op jit(solution)/shard_map/pallas_call | solution.py:749

commit v5 on v4

--- a/solution.py
+++ b/solution.py
@@ -69,13 +69,13 @@
     sides = [1] if depth == 2 else [1, -1]
     ends = (-1, 1)
     groups = [
-        [((0, 0, dz), HALF) for dz in sides],
-        [((dx, 0, 0), 2 * CELLS) for dx in ends],
-        [((0, dy, 0), 2 * CELLS) for dy in ends],
-        [((dx, 0, dz), CELLS) for dz in sides for dx in ends],
         [((0, dy, dz), CELLS // 2) for dz in sides for dy in ends],
         [((dx, dy, 0), 1) for dx in ends for dy in ends],
         [((dx, dy, dz), 1) for dz in sides for dx in ends for dy in ends],
+        [((0, dy, 0), 2 * CELLS) for dy in ends],
+        [((dx, 0, dz), CELLS) for dz in sides for dx in ends],
+        [((dx, 0, 0), 2 * CELLS) for dx in ends],
+        [((0, 0, dz), HALF) for dz in sides],
     ]
     plan, at = [], 0
     for step, rows in [entry for group in groups for entry in group]:
@@ -625,11 +625,22 @@
     reply = remote(back_mail, back_inbox, send_b.at[1], recv_b.at[1], swapped)
     reply.start()
     partial = mm_exact_a(hot_j, placed(there, [-g for g in grad]))
-    part[...] = partial
-    for step, at, rows in by_reach(plan):
-        span = pl.ds(at, rows)
-        copy = remote(part.at[span], got.at[span], send_b.at[0], recv_b.at[0], holder(step))
-        unless_mine(step, copy.start)
+    early = max(at + rows for (_, dy, _), at, rows in plan if dy)
+
+    def give(entries):
+        for step, at, rows in entries:
+            span = pl.ds(at, rows)
+            copy = remote(
+                part.at[span], got.at[span], send_b.at[0], recv_b.at[0], holder(step)
+            )
+            unless_mine(step, copy.start)
+
+    ranked = by_reach(plan)
+    first_rows = -(-early // 8) * 8
+    part[pl.ds(0, first_rows), :] = partial[0:first_rows]
+    give([entry for entry in ranked if entry[0][1]])
+    part[pl.ds(first_rows, halo_rows - first_rows), :] = partial[first_rows:]
+    give([entry for entry in ranked if not entry[0][1]])
 
     reply.wait_recv()
     answer = back_inbox[...]

time: 17.1 us -> 17.1 us (level)
  no operation moved by 1% of the time
where the time goes in v5:
time: 17.1 us; the launch traced here: 16.9 us
  Pallas kernels  15.6 us (91%)
  between operations  1.29 us (8%)
    pallas_call x1, Pallas kernels, local(): pl.pallas_call(body, out_shape=pltpu.VMEM((CELLS * CELLS + 8, LANES), jnp...  14.9 us
    pallas_call x1, Pallas kernels, local(): pl.pallas_call(unpack_body, out_shape=(jax.ShapeDtypeStruct(centres.shape...  0.7 us

profile of v5, /device:TPU:0, one launch (start us, length us, event | category | flops | bytes accessed | tf_op | source)
XLA Modules:
  0.0 16.9 jit_solution(2251083161718206144)
XLA Ops:
  1.3 14.9 %shard_map.122.result = f32[72,128]{1,0:T(8,128)S(1)} custom-call(f32[1,1,4608]{2,1,0:T(1,128)} %refs_0_.1, s32[1,1,1536]{2,1,0:T(1,128)} %refs_1_.1, s32[1,1,16]{2,1,0:T(1,128)} %refs_2_.1, s32[1,1,512]{2,1,0:T(1,128)} %refs_3_.1, s32[1,1,16]{2,1,0:T(1,128)} %refs_4_.1, s32[1,1,1]{2,1,0:T(1,128)S(6)} %copy.13.refs_5_, f32[12,64]{1,0:T(8,128)} %refs_6_.1, ...), custom_call_target="tpu_custom_call" | custom-call | tf_op jit(solution)/shard_map/pallas_call | solution.py:748
  16.2 0.7 %shard_map.123 = (f32[1,1,16]{2,1,0:T(1,128)}, f32[1,1,4608]{2,1,0:T(1,128)}) custom-call(f32[72,128]{1,0:T(8,128)S(1)} %shard_map.122.result), custom_call_target="tpu_custom_call" | custom-call | tf_op jit(solution)/shard_map/pallas_call | solution.py:760

commit v6 on v5

--- a/solution.py
+++ b/solution.py
@@ -124,7 +124,7 @@
                 lat_hbm, env_hbm, out_hbm, readout_hbm, result,
                 disp, spec, cen, nbr, cnt, alive, w_two, w_lat, w_env, w_out_t, readout,
                 table, pack, ztable, zpack, note, inbox, mail, mail_in, back_mail, back_inbox, halo, part, got,
-                send_a, recv_a, send_b, recv_b, load):
+                recv_a, recv_b, load, send_a, send_b):
     loads = [
         pltpu.make_async_copy(src, dst, load.at[at])
         for at, (src, dst) in enumerate(
@@ -736,8 +736,10 @@
 
         def body(*refs):
             pl.run_scoped(
-                lambda load: kernel_body(sizes, plan, *refs, load),
+                lambda *local_sems: kernel_body(sizes, plan, *refs, *local_sems),
                 pltpu.SemaphoreType.DMA((len(args),)),
+                pltpu.SemaphoreType.DMA((3,)),
+                pltpu.SemaphoreType.DMA((2,)),
             )
 
         sizes_vmem = [
@@ -752,8 +754,7 @@
             out_specs=vmem,
             scratch_shapes=[pltpu.VMEM(x.shape, x.dtype) for x in args]
             + [pltpu.VMEM(shape, jnp.float32) for shape in sizes_vmem]
-            + [pltpu.SemaphoreType.DMA((3,))] * 2
-            + [pltpu.SemaphoreType.DMA((2,))] * 2,
+            + [pltpu.SemaphoreType.DMA((3,)), pltpu.SemaphoreType.DMA((2,))],
             compiler_params=pltpu.CompilerParams(collective_id=0, has_side_effects=True),
         )(*args)
         result = pltpu.with_memory_space_constraint(result, pltpu.VMEM)

time: 17.1 us -> 17 us (level)
  no operation moved by 1% of the time
where the time goes in v6:
time: 17 us; the launch traced here: 16.9 us
  Pallas kernels  15.6 us (92%)
  between operations  1.29 us (8%)
    pallas_call x1, Pallas kernels, local(): pl.pallas_call(body, out_shape=pltpu.VMEM((CELLS * CELLS + 8, LANES), jnp...  14.9 us
    pallas_call x1, Pallas kernels, local(): pl.pallas_call(unpack_body, out_shape=(jax.ShapeDtypeStruct(centres.shape...  0.7 us

profile of v6, /device:TPU:0, one launch (start us, length us, event | category | flops | bytes accessed | tf_op | source)
XLA Modules:
  0.0 16.9 jit_solution(1898590407234545404)
XLA Ops:
  1.3 14.9 %shard_map.122.result = f32[72,128]{1,0:T(8,128)S(1)} custom-call(f32[1,1,4608]{2,1,0:T(1,128)} %refs_0_.1, s32[1,1,1536]{2,1,0:T(1,128)} %refs_1_.1, s32[1,1,16]{2,1,0:T(1,128)} %refs_2_.1, s32[1,1,512]{2,1,0:T(1,128)} %refs_3_.1, s32[1,1,16]{2,1,0:T(1,128)} %refs_4_.1, s32[1,1,1]{2,1,0:T(1,128)S(6)} %copy.13.refs_5_, f32[12,64]{1,0:T(8,128)} %refs_6_.1, ...), custom_call_target="tpu_custom_call" | custom-call | tf_op jit(solution)/shard_map/pallas_call | solution.py:750
  16.2 0.7 %shard_map.123 = (f32[1,1,16]{2,1,0:T(1,128)}, f32[1,1,4608]{2,1,0:T(1,128)}) custom-call(f32[72,128]{1,0:T(8,128)S(1)} %shard_map.122.result), custom_call_target="tpu_custom_call" | custom-call | tf_op jit(solution)/shard_map/pallas_call | solution.py:761
